TPU v7x, 32 devices: a whole 2x2x4 slice. The times are simulated.
32 devices in a mesh: dx: 2 (over x), dy: 16 (over z, y, core).
Axes of the slice: x: 2, y: 2, z: 4, core: 2. Of those that a mesh axis runs over, the one named last changes fastest.
Arguments:
- seg_mid: float32 [2, 16, 3, 4096], P('dx', 'dy'), may hold values from 0 to 1
- seg_line: float32 [2, 16, 3, 4096], P('dx', 'dy'), may hold values from -0.3 to 0.3
- seg_burgers: float32 [2, 16, 3, 4096], P('dx', 'dy'), may hold values from -5 to 5
- seg_cell: int32 [2, 16, 4096], P('dx', 'dy'), may hold values from 0 to 71, as said below
- seg_node: int32 [2, 16, 2, 4096], P('dx', 'dy'), may hold values from 0 to 4607, as said below
- ghost_list: int32 [2, 16, 8, 2], P('dx', 'dy'), may hold values from 0 to 31
- ghost_count: int32 [2, 16, 8], P('dx', 'dy'), may hold values from 1 to 2
- pair_list: int32 [2, 16, 32, 12], P('dx', 'dy'), may hold values from 0 to 47, as said below
- pair_count: int32 [2, 16, 32], P('dx', 'dy'), may hold values from 1 to 12
Outputs:
- node_force: float32 [2, 16, 3, 512], P('dx', 'dy')
- cell_moments: float32 [315, 256], P(None, ('dx', 'dy'))
Inputs may be any that keep to these rules, and one draw needn't show every extreme that they name: `seg_node`: each entry is d * 512 + m with m a node of the domain at offset (a, b) from the segment's domain, d = 3 (a + 1) + (b + 1), a and b in -1, 0, 1; d = 4 is the domain itself. `seg_cell`: each entry is d * 8 + c with c a cell owned by the domain at offset (a, b) from the segment's domain, d = 3 (a + 1) + (b + 1), a and b in -1, 0, 1; d = 4 is the domain itself. `pair_list`: the entries of one tile's list are distinct.
All inputs are finite; a program needn't handle non-finite values.
Results may differ from a plain program's by a relative error of at most 0.0003.
Values sent between devices are 32-bit elements; how exact they have to be, the bound alone decides.
A program may use at most 64 MiB of HBM per device.

v0:
```python
import jax
import jax.numpy as jnp
import numpy as np
from jax import lax
from jax.sharding import PartitionSpec as P

TILE = 128
GHOST = 2
NP = 12
NODE_DEV = 512
CELL_DEV = 8


core_radius = 0.1
shear_scale = 0.25
highest = lax.Precision.HIGHEST
neighbour_offsets = ((-1, -1), (-1, 0), (-1, 1), (0, -1), (0, 1), (1, -1), (1, 0), (1, 1))


def passed_along(block, axis, distance):
    devices = range(lax.axis_size(axis))
    route = [((i - distance) % len(devices), i) for i in devices]
    return lax.ppermute(block, axis, route)


def exponent_table():
    exponent_rows = []
    for degree in range(5):
        for first_power in range(degree, -1, -1):
            for second in range(degree - first_power, -1, -1):
                exponent_rows.append((first_power, second, degree - first_power - second))
    return np.array(exponent_rows, dtype=np.int32)


def moment_terms(midpoint, line_vector, burgers):
    scaled = 2.0 * (midpoint - 0.5)
    powers = jnp.stack(
        [jnp.ones_like(scaled), scaled, scaled * scaled, scaled**3, scaled**4], axis=1
    )
    exponents = exponent_table()
    monomial = powers[0, exponents[:, 0]] * powers[1, exponents[:, 1]] * powers[2, exponents[:, 2]]
    products = (burgers[:, None, :] * line_vector[None, :, :]).reshape(9, -1)
    return (products[:, None, :] * monomial[None, :, :]).reshape(9 * monomial.shape[0], -1)


def pair_stress(field_tiles, source_tiles, valid_weight):
    separation = [
        field_tiles[component][:, :, None] - source_tiles[component][:, None, :]
        for component in range(3)
    ]
    line_source = source_tiles[3:6]
    burgers_source = source_tiles[6:9]
    cross_source = [
        burgers_source[1] * line_source[2] - burgers_source[2] * line_source[1],
        burgers_source[2] * line_source[0] - burgers_source[0] * line_source[2],
        burgers_source[0] * line_source[1] - burgers_source[1] * line_source[0],
    ]
    cross_source = [entry_value[:, None, :] for entry_value in cross_source]
    radius_sq = separation[0] ** 2 + separation[1] ** 2 + separation[2] ** 2 + core_radius**2
    inverse = 1.0 / jnp.sqrt(radius_sq)
    weight = shear_scale * valid_weight[:, None, None] * inverse / radius_sq
    projection = (
        separation[0] * cross_source[0]
        + separation[1] * cross_source[1]
        + separation[2] * cross_source[2]
    )
    diagonal_term = projection * (1.0 + 1.5 * core_radius**2 / radius_sq)
    entries = []
    for first_axis, second_axis in ((0, 0), (1, 1), (2, 2), (0, 1), (0, 2), (1, 2)):
        entry_value = (
            separation[first_axis] * cross_source[second_axis]
            + separation[second_axis] * cross_source[first_axis]
            - 3.0 * projection * separation[first_axis] * separation[second_axis] / radius_sq
        )
        if first_axis == second_axis:
            entry_value = entry_value + diagonal_term
        entries.append(jnp.sum(weight * entry_value, axis=2))
    return jnp.stack(entries)


def segment_force(stress, own_columns):
    line_vector = own_columns[3:6]
    burgers = own_columns[6:9]
    traction = [
        stress[0] * burgers[0] + stress[3] * burgers[1] + stress[4] * burgers[2],
        stress[3] * burgers[0] + stress[1] * burgers[1] + stress[5] * burgers[2],
        stress[4] * burgers[0] + stress[5] * burgers[1] + stress[2] * burgers[2],
    ]
    return jnp.stack(
        [
            traction[1] * line_vector[2] - traction[2] * line_vector[1],
            traction[2] * line_vector[0] - traction[0] * line_vector[2],
            traction[0] * line_vector[1] - traction[1] * line_vector[0],
        ]
    )


def on_device(
    seg_mid,
    seg_line,
    seg_burgers,
    seg_cell,
    seg_node,
    ghost_list,
    ghost_count,
    pair_list,
    pair_count,
):
    seg_data = jnp.concatenate([seg_mid[0, 0], seg_line[0, 0], seg_burgers[0, 0]], axis=0)
    own_count = seg_data.shape[1] // TILE
    own_tiles = seg_data.reshape(9, own_count, TILE).transpose(1, 0, 2)
    packets = own_tiles[ghost_list[0, 0]]
    slot_valid = (jnp.arange(GHOST, dtype=jnp.int32)[None, :] < ghost_count[0, 0][:, None]).astype(
        jnp.float32
    )
    packets = packets * slot_valid[:, :, None, None]
    along_x = [
        passed_along(outgoing, "dx", stride)
        for stride, outgoing in ((1, packets[5:8]), (-1, packets[0:3]))
    ]
    from_left = along_x[0]
    from_right = along_x[1]
    upward = jnp.stack([packets[4], from_left[2], from_right[2]])
    downward = jnp.stack([packets[3], from_left[0], from_right[0]])
    along_y = [
        passed_along(outgoing, "dy", stride) for stride, outgoing in ((1, upward), (-1, downward))
    ]
    from_below = along_y[0]
    from_above = along_y[1]
    terms = moment_terms(seg_mid[0, 0], seg_line[0, 0], seg_burgers[0, 0])
    cell_columns = jnp.arange(9 * CELL_DEV, dtype=jnp.int32)
    membership = (seg_cell[0, 0][:, None] == cell_columns[None, :]).astype(jnp.float32)
    moment_partial = jnp.dot(
        terms, membership, precision=highest, preferred_element_type=jnp.float32
    )
    cell_grid = moment_partial.reshape(moment_partial.shape[0], 3, 3, CELL_DEV)
    cell_rows = [
        passed_along(cell_grid[:, :, column], "dy", stride) for stride, column in ((1, 2), (-1, 0))
    ]
    cell_middle = cell_grid[:, :, 1] + cell_rows[0] + cell_rows[1]
    cell_cols = [
        passed_along(cell_middle[:, column], "dx", stride) for stride, column in ((1, 2), (-1, 0))
    ]
    cell_moments = cell_middle[:, 1] + cell_cols[0] + cell_cols[1]
    groups = [
        from_below[1],
        from_left[1],
        from_above[1],
        from_below[0],
        from_above[0],
        from_below[2],
        from_right[1],
        from_above[2],
    ]
    shifted = []
    for group_index in range(8):
        first_shift, second_shift = neighbour_offsets[group_index]
        offset_rows = jnp.array([first_shift, second_shift, 0, 0, 0, 0, 0, 0, 0], jnp.float32)
        shifted.append(groups[group_index] + offset_rows[None, :, None])
    source_pool = jnp.concatenate([own_tiles] + shifted, axis=0)
    own_columns = own_tiles.transpose(1, 0, 2)
    pair_rows = pair_list[0, 0]
    pair_limit = pair_count[0, 0]

    def add_slot(stress_total, slot_index):
        source_tiles = source_pool[pair_rows[:, slot_index]].transpose(1, 0, 2)
        valid_weight = (slot_index < pair_limit).astype(jnp.float32)
        return (stress_total + pair_stress(own_columns, source_tiles, valid_weight), None)

    stress_total, unused = lax.scan(
        add_slot, jnp.zeros((6, own_count, TILE), jnp.float32), jnp.arange(NP, dtype=jnp.int32)
    )
    force = segment_force(stress_total, own_columns).reshape(3, own_count * TILE)
    node_columns = jnp.arange(9 * NODE_DEV, dtype=jnp.int32)
    node_ends = seg_node[0, 0]
    incidence = (node_ends[0][:, None] == node_columns[None, :]).astype(jnp.float32) + (
        node_ends[1][:, None] == node_columns[None, :]
    ).astype(jnp.float32)
    node_partial = jnp.dot(
        0.5 * force, incidence, precision=highest, preferred_element_type=jnp.float32
    )
    node_grid = node_partial.reshape(3, 3, 3, NODE_DEV)
    along_rows = [
        passed_along(node_grid[:, row], "dx", stride) for stride, row in ((1, 2), (-1, 0))
    ]
    partial_mid = node_grid[:, 1] + along_rows[0] + along_rows[1]
    along_cols = [
        passed_along(partial_mid[:, column], "dy", stride) for stride, column in ((1, 2), (-1, 0))
    ]
    node_total = partial_mid[:, 1] + along_cols[0] + along_cols[1]
    return (node_total[None, None], cell_moments)


def solution(mesh):
    in_specs = (
        P("dx", "dy", None, None),
        P("dx", "dy", None, None),
        P("dx", "dy", None, None),
        P("dx", "dy", None),
        P("dx", "dy", None, None),
        P("dx", "dy", None, None),
        P("dx", "dy", None),
        P("dx", "dy", None, None),
        P("dx", "dy", None),
    )
    out_specs = (P("dx", "dy", None, None), P(None, ("dx", "dy")))
    return jax.shard_map(
        on_device, mesh=mesh, in_specs=in_specs, out_specs=out_specs, check_vma=False
    )
```

profile of v0, /device:TPU:0, one launch (start us, length us, event | category | flops | bytes accessed | tf_op | source)
XLA Modules:
  0.0 264.8 jit_solution(2471241427780326510)
XLA Ops:
  3.9 3.0 %collective-permute-start = (f32[3,2,9,128]{3,2,1,0:T(8,128)S(1)}, f32[3,2,9,128]{3,2,1,0:T(8,128)S(1)}, u32[]{:S(2)}, u32[]{:S(2)}) collective-permute-start(f32[3,2,9,128]{3,2,1,0:T(8,128)S(1)} %get-tuple-element.106), channel_id=1, source_target_pairs={{16,0},{0,16},{17,1},{1,17},{18,2},{2,18},{19,3},{3,19},{20,4},{4,... | collective-permute-start | bytes 82952 | tf_op jit(solution)/shard_map/ppermute | solution.py:23
  10.6 2.0 gather_fusion.2
  12.7 2.0 gather_fusion.3
  14.7 2.0 gather_fusion.4
  17.0 3.3 %broadcast_multiply_fusion = f32[9,35,4096]{2,1,0:T(8,128)} fusion(f32[35,4096]{1,0:T(8,128)S(1)} %multiply_multiply_fusion, f32[9,4096]{1,0:T(8,128)S(1)} %mul.423), kind=kLoop, calls=%fused_computation.95 | loop fusion | flops 1290240 | bytes 5881856 | tf_op jit(solution)/shard_map/mul | solution.py:43
  20.2 7.3 %reshape.357 = f32[315,4096,1,1]{1,0,2,3:T(8,128)} reshape(f32[9,35,4096]{2,1,0:T(8,128)} %broadcast_multiply_fusion) | data formatting | bytes 10321920 | tf_op jit(solution)/shard_map/mul | solution.py:43
  27.6 5.3 %fusion.50 = f32[315,3,3,8]{0,3,2,1:T(8,128)S(1)} fusion(f32[315,4096,1,1]{1,0,2,3:T(8,128)} %reshape.357, s32[3,3,8]{2,1,0:T(4,128)S(1)} %multiply_add_fusion.4, s32[4096]{0:T(1024)S(1)} %bitcast.234), kind=kOutput, calls=%fused_computation.93 | convolution fusion | flops 1115062272 | bytes 5268352 | tf_op jit(solution)/shard_map/dot_general | solution.py:133
  33.0 4.4 %collective-permute-start.9 = (f32[315,3,8]{0,2,1:T(8,128)S(1)}, f32[315,3,8]{0,2,1:T(8,128)S(1)}, u32[]{:S(2)}, u32[]{:S(2)}) collective-permute-start(f32[315,3,8]{0,2,1:T(8,128)S(1)} %get-tuple-element.109), channel_id=1, source_target_pairs={{1,0},{2,1},{3,2},{4,3},{5,4},{6,5},{7,6},{8,7},{9,8},{10,9},{11,1... | collective-permute-start | bytes 90728 | tf_op jit(solution)/shard_map/ppermute | solution.py:23
  37.8 4.4 %collective-permute-start.3 = (f32[3,2,9,128]{3,2,1,0:T(8,128)S(1)}, f32[3,2,9,128]{3,2,1,0:T(8,128)S(1)}, u32[]{:S(2)}, u32[]{:S(2)}) collective-permute-start(f32[3,2,9,128]{3,2,1,0:T(8,128)S(1)} %pad_maximum_fusion.2), channel_id=1, source_target_pairs={{1,0},{2,1},{3,2},{4,3},{5,4},{6,5},{7,6},{8,7},{9,8},{10,9},{11,1... | collective-permute-start | bytes 82952 | tf_op jit(solution)/shard_map/ppermute | solution.py:23
  44.6 139.4 %while.11 = (s32[]{:T(128)}, f32[6,32,128]{2,1,0:T(8,128)S(1)}, f32[9,32,128]{2,1,0:T(8,128)S(1)}, s32[12]{0:T(128)S(1)}, s32[32,12]{0,1:T(8,128)S(1)}, /*index=...) while((s32[]{:T(128)}, f32[6,32,128]{2,1,0:T(8,128)S(1)}, ...), condition=%wide.region_7.8_spmd.clone, body=%wide.region_0.7_spmd.clone.sunk | while | flops 35714212 | bytes 1381413 | solution.py:170
  48.6 7.5 %fusion.99 = (f32[32,128]{1,0:T(8,128)S(1)}, f32[32,128]{1,0:T(8,128)S(1)}, f32[32,128]{1,0:T(8,128)S(1)}, f32[32,128]{1,0:T(8,128)S(1)}, f32[32,128]{1,0:T(8,128)S(1)}, /*index=5*/f32[32,128]{1,0:T(8,128)S(1)}) fusion(f32[32,128]{1,0:T(8,128)S(1)} %bitcast.211, f32[32,128]{1,0:T(8,128)S(1)} %bitcast.210, f32[32,128]{1,0:T(8,128)S(1)} %bitcast.212, ...), kind=kLoop, calls=%fused_computation.62.clone.1 | loop fusion | flops 35627008 | bytes 245888 | tf_op jit(solution)/shard_map/while/body/eval_jaxpr/reduce_sum | solution.py:77
  60.2 7.5 %fusion.99 = (f32[32,128]{1,0:T(8,128)S(1)}, f32[32,128]{1,0:T(8,128)S(1)}, f32[32,128]{1,0:T(8,128)S(1)}, f32[32,128]{1,0:T(8,128)S(1)}, f32[32,128]{1,0:T(8,128)S(1)}, /*index=5*/f32[32,128]{1,0:T(8,128)S(1)}) fusion(f32[32,128]{1,0:T(8,128)S(1)} %bitcast.211, f32[32,128]{1,0:T(8,128)S(1)} %bitcast.210, f32[32,128]{1,0:T(8,128)S(1)} %bitcast.212, ...), kind=kLoop, calls=%fused_computation.62.clone.1 | loop fusion | flops 35627008 | bytes 245888 | tf_op jit(solution)/shard_map/while/body/eval_jaxpr/reduce_sum | solution.py:77
  71.8 7.5 %fusion.99 = (f32[32,128]{1,0:T(8,128)S(1)}, f32[32,128]{1,0:T(8,128)S(1)}, f32[32,128]{1,0:T(8,128)S(1)}, f32[32,128]{1,0:T(8,128)S(1)}, f32[32,128]{1,0:T(8,128)S(1)}, /*index=5*/f32[32,128]{1,0:T(8,128)S(1)}) fusion(f32[32,128]{1,0:T(8,128)S(1)} %bitcast.211, f32[32,128]{1,0:T(8,128)S(1)} %bitcast.210, f32[32,128]{1,0:T(8,128)S(1)} %bitcast.212, ...), kind=kLoop, calls=%fused_computation.62.clone.1 | loop fusion | flops 35627008 | bytes 245888 | tf_op jit(solution)/shard_map/while/body/eval_jaxpr/reduce_sum | solution.py:77
  83.4 7.5 %fusion.99 = (f32[32,128]{1,0:T(8,128)S(1)}, f32[32,128]{1,0:T(8,128)S(1)}, f32[32,128]{1,0:T(8,128)S(1)}, f32[32,128]{1,0:T(8,128)S(1)}, f32[32,128]{1,0:T(8,128)S(1)}, /*index=5*/f32[32,128]{1,0:T(8,128)S(1)}) fusion(f32[32,128]{1,0:T(8,128)S(1)} %bitcast.211, f32[32,128]{1,0:T(8,128)S(1)} %bitcast.210, f32[32,128]{1,0:T(8,128)S(1)} %bitcast.212, ...), kind=kLoop, calls=%fused_computation.62.clone.1 | loop fusion | flops 35627008 | bytes 245888 | tf_op jit(solution)/shard_map/while/body/eval_jaxpr/reduce_sum | solution.py:77
  95.0 7.5 %fusion.99 = (f32[32,128]{1,0:T(8,128)S(1)}, f32[32,128]{1,0:T(8,128)S(1)}, f32[32,128]{1,0:T(8,128)S(1)}, f32[32,128]{1,0:T(8,128)S(1)}, f32[32,128]{1,0:T(8,128)S(1)}, /*index=5*/f32[32,128]{1,0:T(8,128)S(1)}) fusion(f32[32,128]{1,0:T(8,128)S(1)} %bitcast.211, f32[32,128]{1,0:T(8,128)S(1)} %bitcast.210, f32[32,128]{1,0:T(8,128)S(1)} %bitcast.212, ...), kind=kLoop, calls=%fused_computation.62.clone.1 | loop fusion | flops 35627008 | bytes 245888 | tf_op jit(solution)/shard_map/while/body/eval_jaxpr/reduce_sum | solution.py:77
  106.7 7.5 %fusion.99 = (f32[32,128]{1,0:T(8,128)S(1)}, f32[32,128]{1,0:T(8,128)S(1)}, f32[32,128]{1,0:T(8,128)S(1)}, f32[32,128]{1,0:T(8,128)S(1)}, f32[32,128]{1,0:T(8,128)S(1)}, /*index=5*/f32[32,128]{1,0:T(8,128)S(1)}) fusion(f32[32,128]{1,0:T(8,128)S(1)} %bitcast.211, f32[32,128]{1,0:T(8,128)S(1)} %bitcast.210, f32[32,128]{1,0:T(8,128)S(1)} %bitcast.212, ...), kind=kLoop, calls=%fused_computation.62.clone.1 | loop fusion | flops 35627008 | bytes 245888 | tf_op jit(solution)/shard_map/while/body/eval_jaxpr/reduce_sum | solution.py:77
  118.3 7.5 %fusion.99 = (f32[32,128]{1,0:T(8,128)S(1)}, f32[32,128]{1,0:T(8,128)S(1)}, f32[32,128]{1,0:T(8,128)S(1)}, f32[32,128]{1,0:T(8,128)S(1)}, f32[32,128]{1,0:T(8,128)S(1)}, /*index=5*/f32[32,128]{1,0:T(8,128)S(1)}) fusion(f32[32,128]{1,0:T(8,128)S(1)} %bitcast.211, f32[32,128]{1,0:T(8,128)S(1)} %bitcast.210, f32[32,128]{1,0:T(8,128)S(1)} %bitcast.212, ...), kind=kLoop, calls=%fused_computation.62.clone.1 | loop fusion | flops 35627008 | bytes 245888 | tf_op jit(solution)/shard_map/while/body/eval_jaxpr/reduce_sum | solution.py:77
  129.9 7.5 %fusion.99 = (f32[32,128]{1,0:T(8,128)S(1)}, f32[32,128]{1,0:T(8,128)S(1)}, f32[32,128]{1,0:T(8,128)S(1)}, f32[32,128]{1,0:T(8,128)S(1)}, f32[32,128]{1,0:T(8,128)S(1)}, /*index=5*/f32[32,128]{1,0:T(8,128)S(1)}) fusion(f32[32,128]{1,0:T(8,128)S(1)} %bitcast.211, f32[32,128]{1,0:T(8,128)S(1)} %bitcast.210, f32[32,128]{1,0:T(8,128)S(1)} %bitcast.212, ...), kind=kLoop, calls=%fused_computation.62.clone.1 | loop fusion | flops 35627008 | bytes 245888 | tf_op jit(solution)/shard_map/while/body/eval_jaxpr/reduce_sum | solution.py:77
  141.5 7.5 %fusion.99 = (f32[32,128]{1,0:T(8,128)S(1)}, f32[32,128]{1,0:T(8,128)S(1)}, f32[32,128]{1,0:T(8,128)S(1)}, f32[32,128]{1,0:T(8,128)S(1)}, f32[32,128]{1,0:T(8,128)S(1)}, /*index=5*/f32[32,128]{1,0:T(8,128)S(1)}) fusion(f32[32,128]{1,0:T(8,128)S(1)} %bitcast.211, f32[32,128]{1,0:T(8,128)S(1)} %bitcast.210, f32[32,128]{1,0:T(8,128)S(1)} %bitcast.212, ...), kind=kLoop, calls=%fused_computation.62.clone.1 | loop fusion | flops 35627008 | bytes 245888 | tf_op jit(solution)/shard_map/while/body/eval_jaxpr/reduce_sum | solution.py:77
  153.1 7.5 %fusion.99 = (f32[32,128]{1,0:T(8,128)S(1)}, f32[32,128]{1,0:T(8,128)S(1)}, f32[32,128]{1,0:T(8,128)S(1)}, f32[32,128]{1,0:T(8,128)S(1)}, f32[32,128]{1,0:T(8,128)S(1)}, /*index=5*/f32[32,128]{1,0:T(8,128)S(1)}) fusion(f32[32,128]{1,0:T(8,128)S(1)} %bitcast.211, f32[32,128]{1,0:T(8,128)S(1)} %bitcast.210, f32[32,128]{1,0:T(8,128)S(1)} %bitcast.212, ...), kind=kLoop, calls=%fused_computation.62.clone.1 | loop fusion | flops 35627008 | bytes 245888 | tf_op jit(solution)/shard_map/while/body/eval_jaxpr/reduce_sum | solution.py:77
  164.7 7.5 %fusion.99 = (f32[32,128]{1,0:T(8,128)S(1)}, f32[32,128]{1,0:T(8,128)S(1)}, f32[32,128]{1,0:T(8,128)S(1)}, f32[32,128]{1,0:T(8,128)S(1)}, f32[32,128]{1,0:T(8,128)S(1)}, /*index=5*/f32[32,128]{1,0:T(8,128)S(1)}) fusion(f32[32,128]{1,0:T(8,128)S(1)} %bitcast.211, f32[32,128]{1,0:T(8,128)S(1)} %bitcast.210, f32[32,128]{1,0:T(8,128)S(1)} %bitcast.212, ...), kind=kLoop, calls=%fused_computation.62.clone.1 | loop fusion | flops 35627008 | bytes 245888 | tf_op jit(solution)/shard_map/while/body/eval_jaxpr/reduce_sum | solution.py:77
  176.4 7.5 %fusion.99 = (f32[32,128]{1,0:T(8,128)S(1)}, f32[32,128]{1,0:T(8,128)S(1)}, f32[32,128]{1,0:T(8,128)S(1)}, f32[32,128]{1,0:T(8,128)S(1)}, f32[32,128]{1,0:T(8,128)S(1)}, /*index=5*/f32[32,128]{1,0:T(8,128)S(1)}) fusion(f32[32,128]{1,0:T(8,128)S(1)} %bitcast.211, f32[32,128]{1,0:T(8,128)S(1)} %bitcast.210, f32[32,128]{1,0:T(8,128)S(1)} %bitcast.212, ...), kind=kLoop, calls=%fused_computation.62.clone.1 | loop fusion | flops 35627008 | bytes 245888 | tf_op jit(solution)/shard_map/while/body/eval_jaxpr/reduce_sum | solution.py:77
  184.1 68.3 %fusion.41 = f32[3,3,3,512]{3,0,2,1:T(4,128)S(1)} fusion(s32[4096]{0:T(1024)S(1)} %bitcast.229, s32[3,3,512]{2,1,0:T(4,128)S(1)} %multiply_add_fusion, s32[4096]{0:T(1024)S(1)} %bitcast.228, f32[1,4096]{1,0:T(1,128)S(1)} %bitcast.227, f32[1,4096]{1,0:T(1,128)S(1)} %bitcast.231, f32[1,4096]{1,0:T(1,128)S(1)} %bitcast.230), kind=kOutput, calls=%fused_computation.84 | convolution fusion | flops 773885952 | bytes 155648 | tf_op jit(solution)/shard_map/dot_general | solution.py:179
  258.4 4.4 %collective-permute-start.7 = (f32[3,512]{1,0:T(4,128)S(1)}, f32[3,512]{1,0:T(4,128)S(1)}, u32[]{:S(2)}, u32[]{:S(2)}) collective-permute-start(f32[3,512]{1,0:T(4,128)S(1)} %get-tuple-element.127), channel_id=1, source_target_pairs={{1,0},{2,1},{3,2},{4,3},{5,4},{6,5},{7,6},{8,7},{9,8},{10,9},{11,1... | collective-permute-start | bytes 18440 | tf_op jit(solution)/shard_map/ppermute | solution.py:23
  (277 shorter events, 41.8 us)
Async XLA Ops:
  3.9 33.8 %collective-permute-start = (f32[3,2,9,128]{3,2,1,0:T(8,128)S(1)}, f32[3,2,9,128]{3,2,1,0:T(8,128)S(1)}, u32[]{:S(2)}, u32[]{:S(2)}) collective-permute-start(f32[3,2,9,128]{3,2,1,0:T(8,128)S(1)} %get-tuple-element.106), channel_id=1, source_target_pairs={{16,0},{0,16},{17,1},{1,17},{18,2},{2,18},{19,3},{3,19},{20,4},{4,... | collective-permute-start | bytes 82952 | tf_op jit(solution)/shard_map/ppermute | solution.py:23
  6.9 30.8 %collective-permute-start.1 = (f32[3,2,9,128]{3,2,1,0:T(8,128)S(1)}, f32[3,2,9,128]{3,2,1,0:T(8,128)S(1)}, u32[]{:S(2)}, u32[]{:S(2)}) collective-permute-start(f32[3,2,9,128]{3,2,1,0:T(8,128)S(1)} %get-tuple-element.107), channel_id=1, source_target_pairs={{16,0},{0,16},{17,1},{1,17},{18,2},{2,18},{19,3},{3,19},{20,4},{4,... | collective-permute-start | bytes 82952 | tf_op jit(solution)/shard_map/ppermute | solution.py:23
  27.5 10.1 %copy-start.5 = (f32[1,1,3,4096]{3,1,2,0:T(1,128)S(1)}, f32[1,1,3,4096]{3,1,2,0:T(1,128)}, u32[]{:S(2)}) copy-start(f32[1,1,3,4096]{3,1,2,0:T(1,128)} %param.26) | copy-start | bytes 147460
  27.5 10.1 %copy-start.6 = (s32[1,1,2,4096]{3,2,1,0:T(2,128)S(1)}, s32[1,1,2,4096]{3,2,1,0:T(2,128)}, u32[]{:S(2)}) copy-start(s32[1,1,2,4096]{3,2,1,0:T(2,128)} %param.29) | copy-start | bytes 98308
  27.5 10.2 %copy-start.7 = (s32[1,1,32,12]{2,1,3,0:T(1,128)S(1)}, s32[1,1,32,12]{2,1,3,0:T(1,128)}, u32[]{:S(2)}) copy-start(s32[1,1,32,12]{2,1,3,0:T(1,128)} %param.32) | copy-start | bytes 4612
  27.5 16.5 %copy-start.15 = (f32[9]{0:T(128)S(1)}, f32[9]{0:T(128)}, u32[]{:S(2)}) copy-start(f32[9]{0:T(128)} %constant.84.clone) | copy-start | bytes 112
  27.5 16.6 %copy-start.14 = (f32[9]{0:T(128)S(1)}, f32[9]{0:T(128)}, u32[]{:S(2)}) copy-start(f32[9]{0:T(128)} %constant.85.clone) | copy-start | bytes 112
  27.6 16.6 %copy-start.13 = (f32[9]{0:T(128)S(1)}, f32[9]{0:T(128)}, u32[]{:S(2)}) copy-start(f32[9]{0:T(128)} %constant.86.clone) | copy-start | bytes 112
  27.6 16.7 %copy-start.12 = (f32[9]{0:T(128)S(1)}, f32[9]{0:T(128)}, u32[]{:S(2)}) copy-start(f32[9]{0:T(128)} %constant.87.clone) | copy-start | bytes 112
  27.6 16.7 %copy-start.11 = (f32[9]{0:T(128)S(1)}, f32[9]{0:T(128)}, u32[]{:S(2)}) copy-start(f32[9]{0:T(128)} %constant.88.clone) | copy-start | bytes 112
  27.6 16.8 %copy-start.10 = (f32[9]{0:T(128)S(1)}, f32[9]{0:T(128)}, u32[]{:S(2)}) copy-start(f32[9]{0:T(128)} %constant.89.clone) | copy-start | bytes 112
  27.6 16.9 %copy-start.9 = (f32[9]{0:T(128)S(1)}, f32[9]{0:T(128)}, u32[]{:S(2)}) copy-start(f32[9]{0:T(128)} %constant.90.clone) | copy-start | bytes 112
  27.6 16.9 %copy-start.8 = (f32[9]{0:T(128)S(1)}, f32[9]{0:T(128)}, u32[]{:S(2)}) copy-start(f32[9]{0:T(128)} %constant.91.clone) | copy-start | bytes 112
  27.6 17.0 %copy-start.17 = (s32[1,1,32]{2,1,0:T(1,128)S(1)}, s32[1,1,32]{2,1,0:T(1,128)}, u32[]{:S(2)}) copy-start(s32[1,1,32]{2,1,0:T(1,128)} %param.33) | copy-start | bytes 388
  33.0 9.3 %collective-permute-start.8 = (f32[315,3,8]{0,2,1:T(8,128)S(1)}, f32[315,3,8]{0,2,1:T(8,128)S(1)}, u32[]{:S(2)}, u32[]{:S(2)}) collective-permute-start(f32[315,3,8]{0,2,1:T(8,128)S(1)} %get-tuple-element.108), channel_id=1, source_target_pairs={{15,0},{0,1},{1,2},{2,3},{3,4},{4,5},{5,6},{6,7},{7,8},{8,9},{9,10... | collective-permute-start | bytes 90728 | tf_op jit(solution)/shard_map/ppermute | solution.py:23
  33.0 9.2 %collective-permute-start.9 = (f32[315,3,8]{0,2,1:T(8,128)S(1)}, f32[315,3,8]{0,2,1:T(8,128)S(1)}, u32[]{:S(2)}, u32[]{:S(2)}) collective-permute-start(f32[315,3,8]{0,2,1:T(8,128)S(1)} %get-tuple-element.109), channel_id=1, source_target_pairs={{1,0},{2,1},{3,2},{4,3},{5,4},{6,5},{7,6},{8,7},{9,8},{10,9},{11,1... | collective-permute-start | bytes 90728 | tf_op jit(solution)/shard_map/ppermute | solution.py:23
  37.8 6.3 %collective-permute-start.2 = (f32[3,2,9,128]{3,2,1,0:T(8,128)S(1)}, f32[3,2,9,128]{3,2,1,0:T(8,128)S(1)}, u32[]{:S(2)}, u32[]{:S(2)}) collective-permute-start(f32[3,2,9,128]{3,2,1,0:T(8,128)S(1)} %pad_maximum_fusion.1), channel_id=1, source_target_pairs={{15,0},{0,1},{1,2},{2,3},{3,4},{4,5},{5,6},{6,7},{7,8},{8,9},{9,10... | collective-permute-start | bytes 82952 | tf_op jit(solution)/shard_map/ppermute | solution.py:23
  37.8 6.3 %collective-permute-start.3 = (f32[3,2,9,128]{3,2,1,0:T(8,128)S(1)}, f32[3,2,9,128]{3,2,1,0:T(8,128)S(1)}, u32[]{:S(2)}, u32[]{:S(2)}) collective-permute-start(f32[3,2,9,128]{3,2,1,0:T(8,128)S(1)} %pad_maximum_fusion.2), channel_id=1, source_target_pairs={{1,0},{2,1},{3,2},{4,3},{5,4},{6,5},{7,6},{8,7},{9,8},{10,9},{11,1... | collective-permute-start | bytes 82952 | tf_op jit(solution)/shard_map/ppermute | solution.py:23
  252.4 4.1 %collective-permute-start.4 = (f32[3,3,512]{2,0,1:T(4,128)S(1)}, f32[3,3,512]{2,0,1:T(4,128)S(1)}, u32[]{:S(2)}, u32[]{:S(2)}) collective-permute-start(f32[3,3,512]{2,0,1:T(4,128)S(1)} %get-tuple-element.110), channel_id=1, source_target_pairs={{16,0},{0,16},{17,1},{1,17},{18,2},{2,18},{19,3},{3,19},{20,4},{4,... | collective-permute-start | bytes 55304 | tf_op jit(solution)/shard_map/ppermute | solution.py:23
  254.4 3.8 %collective-permute-start.5 = (f32[3,3,512]{2,0,1:T(4,128)S(1)}, f32[3,3,512]{2,0,1:T(4,128)S(1)}, u32[]{:S(2)}, u32[]{:S(2)}) collective-permute-start(f32[3,3,512]{2,0,1:T(4,128)S(1)} %get-tuple-element.111), channel_id=1, source_target_pairs={{16,0},{0,16},{17,1},{1,17},{18,2},{2,18},{19,3},{3,19},{20,4},{4,... | collective-permute-start | bytes 55304 | tf_op jit(solution)/shard_map/ppermute | solution.py:23
  254.5 8.3 %collective-permute-start.10 = (f32[315,8]{0,1:T(8,128)S(1)}, f32[315,8]{0,1:T(8,128)S(1)}, u32[]{:S(2)}, u32[]{:S(2)}) collective-permute-start(f32[315,8]{0,1:T(8,128)S(1)} %get-tuple-element.122), channel_id=1, source_target_pairs={{16,0},{0,16},{17,1},{1,17},{18,2},{2,18},{19,3},{3,19},{20,4},{4,... | collective-permute-start | bytes 30248 | tf_op jit(solution)/shard_map/ppermute | solution.py:23
  256.5 6.3 %collective-permute-start.11 = (f32[315,8]{0,1:T(8,128)S(1)}, f32[315,8]{0,1:T(8,128)S(1)}, u32[]{:S(2)}, u32[]{:S(2)}) collective-permute-start(f32[315,8]{0,1:T(8,128)S(1)} %get-tuple-element.123), channel_id=1, source_target_pairs={{16,0},{0,16},{17,1},{1,17},{18,2},{2,18},{19,3},{3,19},{20,4},{4,... | collective-permute-start | bytes 30248 | tf_op jit(solution)/shard_map/ppermute | solution.py:23
  258.3 5.8 %collective-permute-start.6 = (f32[3,512]{1,0:T(4,128)S(1)}, f32[3,512]{1,0:T(4,128)S(1)}, u32[]{:S(2)}, u32[]{:S(2)}) collective-permute-start(f32[3,512]{1,0:T(4,128)S(1)} %get-tuple-element.126), channel_id=1, source_target_pairs={{15,0},{0,1},{1,2},{2,3},{3,4},{4,5},{5,6},{6,7},{7,8},{8,9},{9,10... | collective-permute-start | bytes 18440 | tf_op jit(solution)/shard_map/ppermute | solution.py:23
  258.4 5.8 %collective-permute-start.7 = (f32[3,512]{1,0:T(4,128)S(1)}, f32[3,512]{1,0:T(4,128)S(1)}, u32[]{:S(2)}, u32[]{:S(2)}) collective-permute-start(f32[3,512]{1,0:T(4,128)S(1)} %get-tuple-element.127), channel_id=1, source_target_pairs={{1,0},{2,1},{3,2},{4,3},{5,4},{6,5},{7,6},{8,7},{9,8},{10,9},{11,1... | collective-permute-start | bytes 18440 | tf_op jit(solution)/shard_map/ppermute | solution.py:23
  (6 other events, 41.3 us)
where the time goes:
time: 266 us; the launch traced here: 265 us
  other arithmetic  110 us (41%)
  matrix products  73.6 us (28%)
  local copies, waits for them, and re-layouts  30.5 us (11%)
  loops' own time  24.9 us (9%)
  starting transfers between devices  20.7 us (8%)
  waiting for transfers between devices  4.23 us (2%)
    reduce_sum x12, other arithmetic, pair_stress(): entries.append(jnp.sum(weight * entry_value, axis=2))  90.5 us
    dot_general x1, matrix products, on_device(): jnp.dot(0.5 * force, incidence, precision=highest, preferred_element_type...  68.3 us
    another operation x1, loops' own time, on_device(): lax.scan(add_slot, jnp.zeros((6, own_count, TILE), jnp.float32), jnp.aran...  24.9 us
    ppermute x12, starting transfers between devices, passed_along(): return lax.ppermute(block, axis, route)  20.7 us
    mul x12, other arithmetic, pair_stress(): weight = shear_scale * valid_weight[:, None, None] * inverse / radius_sq  7.8 us
    mul x1, local copies, waits for them, and re-layouts, moment_terms(): products[:, None, :] * monomial[None, :, :]  7.28 us
    dynamic_slice x12, local copies, waits for them, and re-layouts, on_device(): lax.scan(add_slot, jnp.zeros((6, own_count, TILE), jnp.float32), jnp.aran...  7.05 us
    gather x12, local copies, waits for them, and re-layouts, add_slot(): source_tiles = source_pool[pair_rows[:, slot_index]].transpose(1, 0, 2)  7.02 us
  transfers between devices with their start and end apart: 12, of which 3 were waited for; matrix products, arithmetic and copies ran while one was open for 10% of the time, Pallas kernels for 0%

commit v1 on v0

v1 whole, which is shorter than its diff:
```python
import functools

import jax
import jax.numpy as jnp
from jax import lax
from jax.experimental import pallas as pl
from jax.experimental.pallas import tpu as pltpu
from jax.sharding import PartitionSpec as P

TILE = 128
GROUP = 8
MONO_ROWS = 40
NODE_ROWS = 16

core_radius = 0.1
shear_scale = 0.25
neighbour_offsets = ((-1, -1), (-1, 0), (-1, 1), (0, -1), (0, 1), (1, -1), (1, 0), (1, 1))


def passed_along(block, axis, distance):
    devices = range(lax.axis_size(axis))
    route = [((i - distance) % len(devices), i) for i in devices]
    return lax.ppermute(block, axis, route)


def exponent_rows():
    rows = []
    for degree in range(5):
        for first in range(degree, -1, -1):
            for second in range(degree - first, -1, -1):
                rows.append((first, second, degree - first - second))
    return rows


def split_two(value):
    high = value.astype(jnp.bfloat16)
    low = (value - high.astype(jnp.float32)).astype(jnp.bfloat16)
    return high, low


def dot_lanes(left, right):
    return lax.dot_general(
        left, right, (((1,), (1,)), ((), ())), preferred_element_type=jnp.float32
    )


def cell_partial(mid_ref, line_ref, burgers_ref, cell_ref, mono_ref, chunk):
    segments = mid_ref.shape[1]
    mono_ref[...] = jnp.zeros_like(mono_ref)
    total = None
    for start in range(0, segments, chunk):
        cols = pl.ds(start, chunk)
        powers = []
        for axis in range(3):
            scaled = 2.0 * (mid_ref[axis : axis + 1, cols] - 0.5)
            square = scaled * scaled
            powers.append((None, scaled, square, square * scaled, square * square))
        for row, exps in enumerate(exponent_rows()):
            value = None
            for axis in range(3):
                if exps[axis]:
                    factor = powers[axis][exps[axis]]
                    value = factor if value is None else value * factor
            if value is None:
                value = jnp.ones((1, chunk), jnp.float32)
            mono_ref[row : row + 1, :] = value
        mono = mono_ref[...]
        highs, lows = [], []
        for beta in range(3):
            b = burgers_ref[beta : beta + 1, cols]
            for gamma in range(3):
                high, low = split_two(mono * (b * line_ref[gamma : gamma + 1, cols]))
                highs.append(high)
                lows.append(low)
        rows = lax.broadcasted_iota(jnp.int32, (TILE, chunk), 0)
        member = jnp.where(rows == cell_ref[0:1, cols], 1.0, 0.0).astype(jnp.bfloat16)
        part = dot_lanes(jnp.concatenate(highs, axis=0), member) + dot_lanes(
            jnp.concatenate(lows, axis=0), member
        )
        total = part if total is None else total + part
    return total


def cells_kernel(mid_ref, line_ref, burgers_ref, cell_ref, out_ref, mono_ref):
    total = cell_partial(mid_ref, line_ref, burgers_ref, cell_ref, mono_ref, mono_ref.shape[1])
    pad = out_ref.shape[1] - total.shape[0]
    total = jnp.concatenate([total, jnp.zeros((pad, TILE), jnp.float32)], axis=0)
    out_ref[...] = total.T[: out_ref.shape[0]]


def spread(mid, line, burgers, source_ref, index):
    g = [
        burgers[1] * line[2] - burgers[2] * line[1],
        burgers[2] * line[0] - burgers[0] * line[2],
        burgers[0] * line[1] - burgers[1] * line[0],
    ]
    rows = list(mid) + [shear_scale * value for value in g]
    rows = rows + [jnp.zeros((2, TILE), jnp.float32)]
    columns = jnp.concatenate(rows, axis=0).T
    for q in range(6):
        source_ref[index, q] = jnp.broadcast_to(columns[:, q : q + 1], (TILE, TILE))


def rows_of(ref, cols):
    return [ref[axis : axis + 1, cols] for axis in range(3)]


def force_kernel(
    list_ref, count_ref, mid_ref, line_ref, burgers_ref, node_ref, ghost_ref, out_ref,
    source_ref, force_ref,
):
    own_count = mid_ref.shape[1] // TILE
    ghost_slots = ghost_ref.shape[0] // 8

    def spread_own(tile, carry):
        cols = pl.ds(pl.multiple_of(tile * TILE, TILE), TILE)
        spread(
            rows_of(mid_ref, cols), rows_of(line_ref, cols), rows_of(burgers_ref, cols),
            source_ref, tile,
        )
        return carry

    lax.fori_loop(0, own_count, spread_own, 0, unroll=2)

    def spread_ghost(slot, carry):
        q = slot // ghost_slots
        d = q + jnp.where(q >= 4, 1, 0)
        shift = ((d // 3 - 1).astype(jnp.float32), (d % 3 - 1).astype(jnp.float32), 0.0)
        rows = [ghost_ref[slot, r : r + 1, :] for r in range(9)]
        mid = [rows[axis] + shift[axis] for axis in range(3)]
        spread(mid, rows[3:6], rows[6:9], source_ref, own_count + slot)
        return carry

    lax.fori_loop(0, 8 * ghost_slots, spread_ghost, 0, unroll=2)

    def one_tile(tile, carry):
        cols = pl.ds(pl.multiple_of(tile * TILE, TILE), TILE)
        x = [jnp.broadcast_to(row, (GROUP, TILE)) for row in rows_of(mid_ref, cols)]

        def one_slot(slot, sums):
            source = list_ref[tile, slot]
            sums = list(sums)
            for k in range(TILE // GROUP):
                part = pl.ds(k * GROUP, GROUP)
                R = [x[m] - source_ref[source, m, part, :] for m in range(3)]
                g = [source_ref[source, 3 + m, part, :] for m in range(3)]
                r2 = (R[0] * R[0] + core_radius**2) + (R[1] * R[1] + R[2] * R[2])
                inverse = lax.rsqrt(r2)
                inverse2 = inverse * inverse
                weight = inverse2 * inverse
                p = R[0] * g[0] + R[1] * g[1] + R[2] * g[2]
                h = p * (1.5 * inverse2)
                a = [g[m] - h * R[m] for m in range(3)]
                A = [weight * R[m] for m in range(3)]
                sums[0] = sums[0] + A[0] * a[0]
                sums[1] = sums[1] + A[1] * a[1]
                sums[2] = sums[2] + A[2] * a[2]
                sums[3] = sums[3] + (A[0] * a[1] + A[1] * a[0])
                sums[4] = sums[4] + (A[0] * a[2] + A[2] * a[0])
                sums[5] = sums[5] + (A[1] * a[2] + A[2] * a[1])
                sums[6] = sums[6] + weight * p
            return tuple(sums)

        zero = jnp.zeros((GROUP, TILE), jnp.float32)
        sums = lax.fori_loop(0, count_ref[tile], one_slot, (zero,) * 7)
        s = [jnp.sum(value, axis=0, keepdims=True) for value in sums]
        diagonal = s[0] + s[1] + s[2] + 1.5 * s[6]
        xx, yy, zz = [2.0 * s[m] + diagonal for m in range(3)]
        xy, xz, yz = s[3:6]
        b = rows_of(burgers_ref, cols)
        l = rows_of(line_ref, cols)
        t = [
            xx * b[0] + xy * b[1] + xz * b[2],
            xy * b[0] + yy * b[1] + yz * b[2],
            xz * b[0] + yz * b[1] + zz * b[2],
        ]
        force_ref[0:1, cols] = 0.5 * (t[1] * l[2] - t[2] * l[1])
        force_ref[1:2, cols] = 0.5 * (t[2] * l[0] - t[0] * l[2])
        force_ref[2:3, cols] = 0.5 * (t[0] * l[1] - t[1] * l[0])
        return carry

    lax.fori_loop(0, own_count, one_tile, 0)

    directions = out_ref.shape[0]
    chunk = 8 * TILE
    quads = NODE_ROWS // 4

    def nodes(step, total):
        cols = pl.ds(pl.multiple_of(step * chunk, chunk), chunk)
        rows = [jnp.broadcast_to(force_ref[m : m + 1, cols], (4, chunk)) for m in range(3)]
        rows = jnp.concatenate(rows + [jnp.zeros((4, chunk), jnp.float32)], axis=0)
        high = rows.astype(jnp.bfloat16).astype(jnp.float32)
        low = rows - high
        place = lax.broadcasted_iota(jnp.int32, (NODE_ROWS, chunk), 0) % quads
        lanes = lax.broadcasted_iota(jnp.int32, (TILE, chunk), 0)
        for end in range(2):
            node = node_ref[end : end + 1, cols]
            member = jnp.where(lanes == node % TILE, 1.0, 0.0).astype(jnp.bfloat16)
            block = node // TILE - place
            left = []
            for value in (high, low):
                for d in range(directions):
                    chosen = jnp.where(block == d * quads, value, 0.0)
                    left.append(chosen.astype(jnp.bfloat16))
            total = total + dot_lanes(jnp.concatenate(left, axis=0), member)
        return total

    total = lax.fori_loop(
        0, mid_ref.shape[1] // chunk, nodes,
        jnp.zeros((2 * directions * NODE_ROWS, TILE), jnp.float32),
    )
    half = directions * NODE_ROWS
    out_ref[...] = (total[:half] + total[half:]).reshape(out_ref.shape)


def vmem():
    return pl.BlockSpec(memory_space=pltpu.VMEM)


def smem():
    return pl.BlockSpec(memory_space=pltpu.SMEM)


def cells_call(mid, line, burgers, cell, cell_rows):
    return pl.pallas_call(
        cells_kernel,
        out_shape=jax.ShapeDtypeStruct((cell_rows, 3 * TILE), jnp.float32),
        in_specs=[vmem()] * 4,
        out_specs=vmem(),
        scratch_shapes=[pltpu.VMEM((MONO_ROWS, 4 * TILE), jnp.float32)],
        compiler_params=pltpu.CompilerParams(vmem_limit_bytes=16 << 20),
        cost_estimate=pl.CostEstimate(flops=10**9, bytes_accessed=10**6, transcendentals=0),
    )(mid, line, burgers, cell)


def force_call(pairs, counts, mid, line, burgers, node, ghosts):
    pool = mid.shape[1] // TILE + ghosts.shape[0]
    return pl.pallas_call(
        force_kernel,
        out_shape=jax.ShapeDtypeStruct((9, NODE_ROWS, TILE), jnp.float32),
        in_specs=[smem()] * 2 + [vmem()] * 5,
        out_specs=vmem(),
        scratch_shapes=[
            pltpu.VMEM((pool, 6, TILE, TILE), jnp.float32),
            pltpu.VMEM((3, mid.shape[1]), jnp.float32),
        ],
        compiler_params=pltpu.CompilerParams(vmem_limit_bytes=40 << 20),
    )(pairs, counts, mid, line, burgers, node, ghosts)


def returned(grid):
    rows = [passed_along(grid[row], "dx", stride) for stride, row in ((1, 2), (-1, 0))]
    middle = grid[1] + rows[0] + rows[1]
    columns = [passed_along(middle[col], "dy", stride) for stride, col in ((1, 2), (-1, 0))]
    return middle[1] + columns[0] + columns[1]


def on_device(
    seg_mid, seg_line, seg_burgers, seg_cell, seg_node,
    ghost_list, ghost_count, pair_list, pair_count,
):
    mid, line, burgers = seg_mid[0, 0], seg_line[0, 0], seg_burgers[0, 0]
    cells = 8
    seg_data = jnp.concatenate([mid, line, burgers], axis=0)
    own_tiles = seg_data.reshape(9, -1, TILE).transpose(1, 0, 2)
    slots = ghost_list.shape[3]
    packets = own_tiles[ghost_list[0, 0]]
    valid = jnp.arange(slots, dtype=jnp.int32)[None, :] < ghost_count[0, 0][:, None]
    packets = packets * valid.astype(jnp.float32)[:, :, None, None]
    from_left = passed_along(packets[5:8], "dx", 1)
    from_right = passed_along(packets[0:3], "dx", -1)
    upward = jnp.stack([packets[4], from_left[2], from_right[2]])
    downward = jnp.stack([packets[3], from_left[0], from_right[0]])
    from_below = passed_along(upward, "dy", 1)
    from_above = passed_along(downward, "dy", -1)
    groups = [
        from_below[1], from_left[1], from_above[1], from_below[0],
        from_above[0], from_below[2], from_right[1], from_above[2],
    ]
    ghosts = jnp.concatenate(groups, axis=0)
    cell_part = cells_call(mid, line, burgers, seg_cell[0], 9 * cells)
    cell_sum = returned(cell_part.reshape(3, 3, cells, -1))
    moments = cell_sum[:, : 9 * MONO_ROWS].reshape(cells, 9, MONO_ROWS)
    moments = moments[:, :, : len(exponent_rows())].reshape(cells, -1).T
    node_part = force_call(pair_list[0, 0], pair_count[0, 0, :], mid, line, burgers, seg_node[0, 0], ghosts)
    node_sum = returned(node_part.reshape(3, 3, NODE_ROWS, TILE))
    force = node_sum[:12].reshape(3, 4 * TILE)
    return (force[None, None], moments)


def solution(mesh):
    in_specs = (
        P("dx", "dy", None, None),
        P("dx", "dy", None, None),
        P("dx", "dy", None, None),
        P("dx", "dy", None),
        P("dx", "dy", None, None),
        P("dx", "dy", None, None),
        P("dx", "dy", None),
        P("dx", "dy", None, None),
        P("dx", "dy", None),
    )
    out_specs = (P("dx", "dy", None, None), P(None, ("dx", "dy")))
    return jax.shard_map(
        on_device, mesh=mesh, in_specs=in_specs, out_specs=out_specs, check_vma=False
    )
```

time: 266 us -> 70.7 us (0.27)
  other arithmetic: 110 us -> 0.27 us
  matrix products: 73.6 us -> 0 us
  Pallas kernels: 0 us -> 37.1 us
  loops' own time: 24.9 us -> 0 us
  local copies, waits for them, and re-layouts: 30.5 us -> 7.36 us
    reduce_sum x12 -> x0, other arithmetic: 90.5 us -> none  [pair_stress(): entries.append(jnp.sum(weight * entry_value, axis=2))]
    dot_general x2 -> x0, matrix products: 73.6 us -> none  [the longest x1 68.3 us: on_device(): jnp.dot(0.5 * force, incidence, precision=highest, preferred_element_type...]
    pallas_call x0 -> x2, Pallas kernels: none -> 37.1 us  [the longest x1 34.9 us: force_call(): pl.pallas_call(force_kernel, out_shape=jax.ShapeDtypeStruct((9, NODE_ROWS...]
    another operation x1 -> x0, loops' own time: 24.9 us -> none  [on_device(): lax.scan(add_slot, jnp.zeros((6, own_count, TILE), jnp.float32), jnp.aran...]
    gather x15 -> x0, local copies, waits for them, and re-layouts: 13.1 us -> none  [the longest x12 7.02 us: add_slot(): source_tiles = source_pool[pair_rows[:, slot_index]].transpose(1, 0, 2)]
    mul x16 -> x1, other arithmetic: 11.3 us -> 0.08 us  [on_device(): packets = packets * valid.astype(jnp.float32)[:, :, None, None]]
    mul x2 -> x0, local copies, waits for them, and re-layouts: 7.36 us -> none  [the longest x1 7.28 us: moment_terms(): products[:, None, :] * monomial[None, :, :]]
    dynamic_slice x12 -> x0, local copies, waits for them, and re-layouts: 7.05 us -> none  [on_device(): lax.scan(add_slot, jnp.zeros((6, own_count, TILE), jnp.float32), jnp.aran...]
  transfers between devices with their start and end apart: 12 -> 12, of which waited for: 3 -> 2; matrix products, arithmetic and copies ran while one was open for 10% -> 1% of each run, Pallas kernels for 0% -> 3%
where the time goes in v1:
time: 70.7 us; the launch traced here: 69.7 us
  Pallas kernels  37.1 us (52%)
  starting transfers between devices  21.8 us (31%)
  local copies, waits for them, and re-layouts  7.36 us (10%)
  waiting for transfers between devices  2.35 us (3%)
  between operations  0.89 us (1%)
    pallas_call x1, Pallas kernels, force_call(): pl.pallas_call(force_kernel, out_shape=jax.ShapeDtypeStruct((9, NODE_ROWS...  34.9 us
    ppermute x12, starting transfers between devices, passed_along(): return lax.ppermute(block, axis, route)  21.8 us
    unnamed x28, local copies, waits for them, and re-layouts  4.3 us
    ppermute x12, waiting for transfers between devices, passed_along(): return lax.ppermute(block, axis, route)  2.35 us
    pallas_call x1, Pallas kernels, cells_call(): pl.pallas_call(cells_kernel, out_shape=jax.ShapeDtypeStruct((cell_rows, 3...  2.13 us
  transfers between devices with their start and end apart: 12, of which 2 were waited for; matrix products, arithmetic and copies ran while one was open for 1% of the time, Pallas kernels for 3%

profile of v1, /device:TPU:0, one launch (start us, length us, event | category | flops | bytes accessed | tf_op | source)
XLA Modules:
  0.0 69.7 jit_solution(2476909156009598224)
XLA Ops:
  0.6 0.8 %copy.18 = f32[3,32,128]{2,0,1:T(4,128)S(1)} copy(f32[3,32,128]{2,1,0:T(8,128)} %bitcast.88) | data formatting | bytes 98304 | tf_op jit(solution)/shard_map/concatenate | solution.py:264
  1.6 0.7 %copy-done.3 = f32[1,1,3,4096]{3,1,2,0:T(1,128)S(1)} copy-done((f32[1,1,3,4096]{3,1,2,0:T(1,128)S(1)}, f32[1,1,3,4096]{3,1,2,0:T(1,128)}, u32[]{:S(2)}) %copy-start.3) | copy-done | bytes 49176
  2.3 0.6 copy-done.7
  3.0 0.1 copy.21
  3.2 0.6 copy-done.8
  4.0 0.6 gather_fusion
  4.6 3.0 %collective-permute-start = (f32[3,2,9,128]{3,2,1,0:T(8,128)S(1)}, f32[3,2,9,128]{3,2,1,0:T(8,128)S(1)}, u32[]{:S(2)}, u32[]{:S(2)}) collective-permute-start(f32[3,2,9,128]{3,2,1,0:T(8,128)S(1)} %get-tuple-element.10), channel_id=1, source_target_pairs={{16,0},{0,16},{17,1},{1,17},{18,2},{2,18},{19,3},{3,19},{20,4},{4,... | collective-permute-start | bytes 82952 | tf_op jit(solution)/shard_map/ppermute | solution.py:23
  7.7 0.1 collective-permute-start.1
  7.8 0.6 copy-done.5
  8.5 0.7 copy-done.2
  9.2 2.1 %shard_map.105 = f32[72,384]{1,0:T(8,128)S(1)} custom-call(f32[3,4096]{1,0:T(4,128)S(1)} %bitcast.78, f32[3,4096]{1,0:T(4,128)S(1)} %get-tuple-element.27.line_ref, f32[3,4096]{1,0:T(4,128)S(1)} %get-tuple-element.26.burgers_ref, s32[1,4096]{1,0:T(1,128)S(1)} %bitcast.83), custom_call_target="tpu_custom_call" | custom-call | flops 1000000000 | bytes 1000000 | tf_op jit(solution)/shard_map/pallas_call | solution.py:225
  11.3 1.4 %collective-permute-start.8 = (f32[3,8,384]{2,1,0:T(8,128)S(1)}, f32[3,8,384]{2,1,0:T(8,128)S(1)}, u32[]{:S(2)}, u32[]{:S(2)}) collective-permute-start(f32[3,8,384]{2,1,0:T(8,128)S(1)} %get-tuple-element.12), channel_id=1, source_target_pairs={{16,0},{0,16},{17,1},{1,17},{18,2},{2,18},{19,3},{3,19},{20,4},{4,... | collective-permute-start | bytes 110600 | tf_op jit(solution)/shard_map/ppermute | solution.py:23
  12.7 0.7 %collective-permute-start.9 = (f32[3,8,384]{2,1,0:T(8,128)S(1)}, f32[3,8,384]{2,1,0:T(8,128)S(1)}, u32[]{:S(2)}, u32[]{:S(2)}) collective-permute-start(f32[3,8,384]{2,1,0:T(8,128)S(1)} %get-tuple-element.13), channel_id=1, source_target_pairs={{16,0},{0,16},{17,1},{1,17},{18,2},{2,18},{19,3},{3,19},{20,4},{4,... | collective-permute-start | bytes 110600 | tf_op jit(solution)/shard_map/ppermute | solution.py:23
  13.4 0.1 copy.17
  13.6 4.4 %collective-permute-start.3 = (f32[3,2,9,128]{3,2,1,0:T(8,128)S(1)}, f32[3,2,9,128]{3,2,1,0:T(8,128)S(1)}, u32[]{:S(2)}, u32[]{:S(2)}) collective-permute-start(f32[3,2,9,128]{3,2,1,0:T(8,128)S(1)} %pad_maximum_fusion.1), channel_id=1, source_target_pairs={{1,0},{2,1},{3,2},{4,3},{5,4},{6,5},{7,6},{8,7},{9,8},{10,9},{11,1... | collective-permute-start | bytes 82952 | tf_op jit(solution)/shard_map/ppermute | solution.py:23
  18.1 1.7 %collective-permute-done.2 = f32[3,2,9,128]{3,2,1,0:T(8,128)S(1)} collective-permute-done((f32[3,2,9,128]{3,2,1,0:T(8,128)S(1)}, f32[3,2,9,128]{3,2,1,0:T(8,128)S(1)}, u32[]{:S(2)}, u32[]{:S(2)}) %collective-permute-start.2) | collective-permute-done | bytes 27680 | tf_op jit(solution)/shard_map/ppermute | solution.py:23
  19.9 0.7 %copy-done = s32[1,1,2,4096]{3,2,1,0:T(2,128)S(1)} copy-done((s32[1,1,2,4096]{3,2,1,0:T(2,128)S(1)}, s32[1,1,2,4096]{3,2,1,0:T(2,128)}, u32[]{:S(2)}) %copy-start) | copy-done | bytes 32792
  20.6 34.9 %shard_map.104 = f32[9,16,128]{2,1,0:T(8,128)S(1)} custom-call(s32[32,12]{1,0:T(8,128)S(1)} %bitcast.80, s32[32]{0:T(128)S(1)} %bitcast.82, f32[3,4096]{1,0:T(4,128)S(1)} %bitcast.79, f32[3,4096]{1,0:T(4,128)S(1)} %get-tuple-element.27.line_ref, f32[3,4096]{1,0:T(4,128)S(1)} %get-tuple-element.26.burgers_ref, s32[2,4096]{1,0:T(2,128)S(1)} %bitcast.81, ...), custom_call_target="tpu_custom_call" | custom-call | tf_op jit(solution)/shard_map/pallas_call | solution.py:238
  55.6 3.1 %collective-permute-start.4 = (f32[3,16,128]{2,1,0:T(8,128)S(1)}, f32[3,16,128]{2,1,0:T(8,128)S(1)}, u32[]{:S(2)}, u32[]{:S(2)}) collective-permute-start(f32[3,16,128]{2,1,0:T(8,128)S(1)} %get-tuple-element.14), channel_id=1, source_target_pairs={{16,0},{0,16},{17,1},{1,17},{18,2},{2,18},{19,3},{3,19},{20,4},{4,... | collective-permute-start | bytes 73736 | tf_op jit(solution)/shard_map/ppermute | solution.py:23
  58.8 4.4 %collective-permute-start.11 = (f32[8,384]{1,0:T(8,128)S(1)}, f32[8,384]{1,0:T(8,128)S(1)}, u32[]{:S(2)}, u32[]{:S(2)}) collective-permute-start(f32[8,384]{1,0:T(8,128)S(1)} %get-tuple-element.21), channel_id=1, source_target_pairs={{1,0},{2,1},{3,2},{4,3},{5,4},{6,5},{7,6},{8,7},{9,8},{10,9},{11,1... | collective-permute-start | bytes 36872 | tf_op jit(solution)/shard_map/ppermute | solution.py:23
  63.3 4.4 %collective-permute-start.7 = (f32[16,128]{1,0:T(8,128)S(1)}, f32[16,128]{1,0:T(8,128)S(1)}, u32[]{:S(2)}, u32[]{:S(2)}) collective-permute-start(f32[16,128]{1,0:T(8,128)S(1)} %get-tuple-element.24), channel_id=1, source_target_pairs={{1,0},{2,1},{3,2},{4,3},{5,4},{6,5},{7,6},{8,7},{9,8},{10,9},{11,1... | collective-permute-start | bytes 24584 | tf_op jit(solution)/shard_map/ppermute | solution.py:23
  67.8 0.7 reshape.85
  68.5 0.5 collective-permute-done.6
  69.1 0.6 broadcast_in_dim_reshape.4
  (59 shorter events, 1.0 us)
Async XLA Ops:
  0.6 0.9 %copy-start.4 = (f32[1,1,3,4096]{3,1,2,0:T(1,128)S(1)}, f32[1,1,3,4096]{3,1,2,0:T(1,128)}, u32[]{:S(2)}) copy-start(f32[1,1,3,4096]{3,1,2,0:T(1,128)} %param.10) | copy-start | bytes 147460
  1.5 0.8 %copy-start.3 = (f32[1,1,3,4096]{3,1,2,0:T(1,128)S(1)}, f32[1,1,3,4096]{3,1,2,0:T(1,128)}, u32[]{:S(2)}) copy-start(f32[1,1,3,4096]{3,1,2,0:T(1,128)} %param.11) | copy-start | bytes 147460
  2.3 0.7 copy-start.7
  3.2 0.7 copy-start.8
  4.6 8.9 %collective-permute-start = (f32[3,2,9,128]{3,2,1,0:T(8,128)S(1)}, f32[3,2,9,128]{3,2,1,0:T(8,128)S(1)}, u32[]{:S(2)}, u32[]{:S(2)}) collective-permute-start(f32[3,2,9,128]{3,2,1,0:T(8,128)S(1)} %get-tuple-element.10), channel_id=1, source_target_pairs={{16,0},{0,16},{17,1},{1,17},{18,2},{2,18},{19,3},{3,19},{20,4},{4,... | collective-permute-start | bytes 82952 | tf_op jit(solution)/shard_map/ppermute | solution.py:23
  7.7 0.8 %copy-start.5 = (f32[1,1,3,4096]{3,1,2,0:T(1,128)S(1)}, f32[1,1,3,4096]{3,1,2,0:T(1,128)}, u32[]{:S(2)}) copy-start(f32[1,1,3,4096]{3,1,2,0:T(1,128)} %param.9) | copy-start | bytes 147460
  7.7 5.9 %collective-permute-start.1 = (f32[3,2,9,128]{3,2,1,0:T(8,128)S(1)}, f32[3,2,9,128]{3,2,1,0:T(8,128)S(1)}, u32[]{:S(2)}, u32[]{:S(2)}) collective-permute-start(f32[3,2,9,128]{3,2,1,0:T(8,128)S(1)} %get-tuple-element.11), channel_id=1, source_target_pairs={{16,0},{0,16},{17,1},{1,17},{18,2},{2,18},{19,3},{3,19},{20,4},{4,... | collective-permute-start | bytes 82952 | tf_op jit(solution)/shard_map/ppermute | solution.py:23
  8.5 0.7 %copy-start.2 = (s32[1,1,4096]{2,1,0:T(1,128)S(1)}, s32[1,1,4096]{2,1,0:T(1,128)}, u32[]{:S(2)}) copy-start(s32[1,1,4096]{2,1,0:T(1,128)} %param.12) | copy-start | bytes 49156
  11.3 6.7 %collective-permute-start.8 = (f32[3,8,384]{2,1,0:T(8,128)S(1)}, f32[3,8,384]{2,1,0:T(8,128)S(1)}, u32[]{:S(2)}, u32[]{:S(2)}) collective-permute-start(f32[3,8,384]{2,1,0:T(8,128)S(1)} %get-tuple-element.12), channel_id=1, source_target_pairs={{16,0},{0,16},{17,1},{1,17},{18,2},{2,18},{19,3},{3,19},{20,4},{4,... | collective-permute-start | bytes 110600 | tf_op jit(solution)/shard_map/ppermute | solution.py:23
  12.7 0.7 %copy-start.6 = (s32[1,1,32,12]{2,1,3,0:T(1,128)S(1)}, s32[1,1,32,12]{2,1,3,0:T(1,128)}, u32[]{:S(2)}) copy-start(s32[1,1,32,12]{2,1,3,0:T(1,128)} %param.16) | copy-start | bytes 4612
  12.7 5.4 %collective-permute-start.9 = (f32[3,8,384]{2,1,0:T(8,128)S(1)}, f32[3,8,384]{2,1,0:T(8,128)S(1)}, u32[]{:S(2)}, u32[]{:S(2)}) collective-permute-start(f32[3,8,384]{2,1,0:T(8,128)S(1)} %get-tuple-element.13), channel_id=1, source_target_pairs={{16,0},{0,16},{17,1},{1,17},{18,2},{2,18},{19,3},{3,19},{20,4},{4,... | collective-permute-start | bytes 110600 | tf_op jit(solution)/shard_map/ppermute | solution.py:23
  13.6 6.3 %collective-permute-start.2 = (f32[3,2,9,128]{3,2,1,0:T(8,128)S(1)}, f32[3,2,9,128]{3,2,1,0:T(8,128)S(1)}, u32[]{:S(2)}, u32[]{:S(2)}) collective-permute-start(f32[3,2,9,128]{3,2,1,0:T(8,128)S(1)} %pad_maximum_fusion), channel_id=1, source_target_pairs={{15,0},{0,1},{1,2},{2,3},{3,4},{4,5},{5,6},{6,7},{7,8},{8,9},{9,10... | collective-permute-start | bytes 82952 | tf_op jit(solution)/shard_map/ppermute | solution.py:23
  13.6 6.2 %collective-permute-start.3 = (f32[3,2,9,128]{3,2,1,0:T(8,128)S(1)}, f32[3,2,9,128]{3,2,1,0:T(8,128)S(1)}, u32[]{:S(2)}, u32[]{:S(2)}) collective-permute-start(f32[3,2,9,128]{3,2,1,0:T(8,128)S(1)} %pad_maximum_fusion.1), channel_id=1, source_target_pairs={{1,0},{2,1},{3,2},{4,3},{5,4},{6,5},{7,6},{8,7},{9,8},{10,9},{11,1... | collective-permute-start | bytes 82952 | tf_op jit(solution)/shard_map/ppermute | solution.py:23
  19.9 0.8 %copy-start = (s32[1,1,2,4096]{3,2,1,0:T(2,128)S(1)}, s32[1,1,2,4096]{3,2,1,0:T(2,128)}, u32[]{:S(2)}) copy-start(s32[1,1,2,4096]{3,2,1,0:T(2,128)} %param.13) | copy-start | bytes 98308
  19.9 0.7 %copy-start.1 = (s32[1,1,32]{2,1,0:T(1,128)S(1)}, s32[1,1,32]{2,1,0:T(1,128)}, u32[]{:S(2)}) copy-start(s32[1,1,32]{2,1,0:T(1,128)} %param.17) | copy-start | bytes 388
  55.6 7.6 %collective-permute-start.4 = (f32[3,16,128]{2,1,0:T(8,128)S(1)}, f32[3,16,128]{2,1,0:T(8,128)S(1)}, u32[]{:S(2)}, u32[]{:S(2)}) collective-permute-start(f32[3,16,128]{2,1,0:T(8,128)S(1)} %get-tuple-element.14), channel_id=1, source_target_pairs={{16,0},{0,16},{17,1},{1,17},{18,2},{2,18},{19,3},{3,19},{20,4},{4,... | collective-permute-start | bytes 73736 | tf_op jit(solution)/shard_map/ppermute | solution.py:23
  58.7 4.5 %collective-permute-start.5 = (f32[3,16,128]{2,1,0:T(8,128)S(1)}, f32[3,16,128]{2,1,0:T(8,128)S(1)}, u32[]{:S(2)}, u32[]{:S(2)}) collective-permute-start(f32[3,16,128]{2,1,0:T(8,128)S(1)} %get-tuple-element.15), channel_id=1, source_target_pairs={{16,0},{0,16},{17,1},{1,17},{18,2},{2,18},{19,3},{3,19},{20,4},{4,... | collective-permute-start | bytes 73736 | tf_op jit(solution)/shard_map/ppermute | solution.py:23
  58.8 9.0 %collective-permute-start.10 = (f32[8,384]{1,0:T(8,128)S(1)}, f32[8,384]{1,0:T(8,128)S(1)}, u32[]{:S(2)}, u32[]{:S(2)}) collective-permute-start(f32[8,384]{1,0:T(8,128)S(1)} %get-tuple-element.22), channel_id=1, source_target_pairs={{15,0},{0,1},{1,2},{2,3},{3,4},{4,5},{5,6},{6,7},{7,8},{8,9},{9,10... | collective-permute-start | bytes 36872 | tf_op jit(solution)/shard_map/ppermute | solution.py:23
  58.8 9.0 %collective-permute-start.11 = (f32[8,384]{1,0:T(8,128)S(1)}, f32[8,384]{1,0:T(8,128)S(1)}, u32[]{:S(2)}, u32[]{:S(2)}) collective-permute-start(f32[8,384]{1,0:T(8,128)S(1)} %get-tuple-element.21), channel_id=1, source_target_pairs={{1,0},{2,1},{3,2},{4,3},{5,4},{6,5},{7,6},{8,7},{9,8},{10,9},{11,1... | collective-permute-start | bytes 36872 | tf_op jit(solution)/shard_map/ppermute | solution.py:23
  63.2 5.8 %collective-permute-start.6 = (f32[16,128]{1,0:T(8,128)S(1)}, f32[16,128]{1,0:T(8,128)S(1)}, u32[]{:S(2)}, u32[]{:S(2)}) collective-permute-start(f32[16,128]{1,0:T(8,128)S(1)} %get-tuple-element.25), channel_id=1, source_target_pairs={{15,0},{0,1},{1,2},{2,3},{3,4},{4,5},{5,6},{6,7},{7,8},{8,9},{9,10... | collective-permute-start | bytes 24584 | tf_op jit(solution)/shard_map/ppermute | solution.py:23
  63.3 5.8 %collective-permute-start.7 = (f32[16,128]{1,0:T(8,128)S(1)}, f32[16,128]{1,0:T(8,128)S(1)}, u32[]{:S(2)}, u32[]{:S(2)}) collective-permute-start(f32[16,128]{1,0:T(8,128)S(1)} %get-tuple-element.24), channel_id=1, source_target_pairs={{1,0},{2,1},{3,2},{4,3},{5,4},{6,5},{7,6},{8,7},{9,8},{10,9},{11,1... | collective-permute-start | bytes 24584 | tf_op jit(solution)/shard_map/ppermute | solution.py:23

commit v2 on v1

--- a/solution.py
+++ b/solution.py
@@ -1,3 +1,5 @@
+import functools
+
 import functools
 
 import jax
@@ -9,18 +11,13 @@
 
 TILE = 128
 GROUP = 8
+CELL_DEV = 8
 MONO_ROWS = 40
 NODE_ROWS = 16
 
 core_radius = 0.1
 shear_scale = 0.25
 neighbour_offsets = ((-1, -1), (-1, 0), (-1, 1), (0, -1), (0, 1), (1, -1), (1, 0), (1, 1))
-
-
-def passed_along(block, axis, distance):
-    devices = range(lax.axis_size(axis))
-    route = [((i - distance) % len(devices), i) for i in devices]
-    return lax.ppermute(block, axis, route)
 
 
 def exponent_rows():
@@ -44,7 +41,16 @@
     )
 
 
-def cell_partial(mid_ref, line_ref, burgers_ref, cell_ref, mono_ref, chunk):
+def folded(value, span, fold):
+    return jnp.where(value >= 6 * span, value - 6 * span, value) if fold else value
+
+
+def owners(n_dx):
+    firsts = (-1, 0) if n_dx == 2 else (-1, 0, 1)
+    return [(a, b) for a in firsts for b in (-1, 0, 1)]
+
+
+def cell_partial(mid_ref, line_ref, burgers_ref, cell_ref, mono_ref, chunk, cells, fold):
     segments = mid_ref.shape[1]
     mono_ref[...] = jnp.zeros_like(mono_ref)
     total = None
@@ -73,7 +79,7 @@
                 highs.append(high)
                 lows.append(low)
         rows = lax.broadcasted_iota(jnp.int32, (TILE, chunk), 0)
-        member = jnp.where(rows == cell_ref[0:1, cols], 1.0, 0.0).astype(jnp.bfloat16)
+        member = jnp.where(rows == folded(cell_ref[0:1, cols], cells, fold), 1.0, 0.0).astype(jnp.bfloat16)
         part = dot_lanes(jnp.concatenate(highs, axis=0), member) + dot_lanes(
             jnp.concatenate(lows, axis=0), member
         )
@@ -81,22 +87,115 @@
     return total
 
 
-def cells_kernel(mid_ref, line_ref, burgers_ref, cell_ref, out_ref, mono_ref):
-    total = cell_partial(mid_ref, line_ref, burgers_ref, cell_ref, mono_ref, mono_ref.shape[1])
-    pad = out_ref.shape[1] - total.shape[0]
-    total = jnp.concatenate([total, jnp.zeros((pad, TILE), jnp.float32)], axis=0)
-    out_ref[...] = total.T[: out_ref.shape[0]]
-
-
-def spread(mid, line, burgers, source_ref, index):
-    g = [
+def neighbour(a, b):
+    n_dx, n_dy = lax.axis_size("dx"), lax.axis_size("dy")
+    i, j = lax.axis_index("dx"), lax.axis_index("dy")
+    return (lax.rem(i + (a + n_dx), n_dx), lax.rem(j + (b + n_dy), n_dy))
+
+
+def greet(offsets):
+    barrier = pltpu.get_barrier_semaphore()
+    for a, b in offsets:
+        pl.semaphore_signal(
+            barrier, inc=1, device_id=neighbour(a, b), device_id_type=pl.DeviceIdType.MESH
+        )
+    return lambda: pl.semaphore_wait(barrier, len(offsets))
+
+
+def start_copies(offsets, source_of, target_of, send_sem, recv_sem):
+    copies = []
+    for index, (a, b) in enumerate(offsets):
+        copy = pltpu.make_async_remote_copy(
+            src_ref=source_of(index),
+            dst_ref=target_of(index),
+            send_sem=send_sem.at[index],
+            recv_sem=recv_sem.at[index],
+            device_id=neighbour(a, b),
+            device_id_type=pl.DeviceIdType.MESH,
+        )
+        copy.start()
+        copies.append(copy)
+    return copies
+
+
+def cross(burgers, line):
+    return [
         burgers[1] * line[2] - burgers[2] * line[1],
         burgers[2] * line[0] - burgers[0] * line[2],
         burgers[0] * line[1] - burgers[1] * line[0],
     ]
-    rows = list(mid) + [shear_scale * value for value in g]
-    rows = rows + [jnp.zeros((2, TILE), jnp.float32)]
-    columns = jnp.concatenate(rows, axis=0).T
+
+
+def pack_kernel(list_ref, count_ref, mid_ref, line_ref, burgers_ref, packet_ref):
+    slots = packet_ref.shape[1]
+    for k, offset in enumerate(neighbour_offsets):
+        for g in range(slots):
+            cols = pl.ds(pl.multiple_of(list_ref[k, g] * TILE, TILE), TILE)
+            valid = jnp.where(g < count_ref[k], 1.0, 0.0)
+            mid = rows_of(mid_ref, cols)
+            mid = [valid * mid[0] - float(offset[0]), valid * mid[1] - float(offset[1]), valid * mid[2]]
+            rows = [valid * row for row in rows_of(burgers_ref, cols)]
+            moment = cross(rows, [valid * row for row in rows_of(line_ref, cols)])
+            rows = mid + [shear_scale * row for row in moment]
+            for r, row in enumerate(rows):
+                packet_ref[k, g, r : r + 1, :] = row
+            packet_ref[k, g, 6:8, :] = jnp.zeros((2, TILE), jnp.float32)
+
+
+def ghost_kernel(
+    cells, fold, packet_ref, mid_ref, line_ref, burgers_ref, cell_ref,
+    ghost_ref, out_ref, mono_ref, packed_ref, send_sem, recv_sem,
+):
+    greet(neighbour_offsets)()
+    copies = start_copies(
+        neighbour_offsets, lambda k: packet_ref.at[k], lambda k: ghost_ref.at[7 - k],
+        send_sem, recv_sem,
+    )
+    total = cell_partial(
+        mid_ref, line_ref, burgers_ref, cell_ref, mono_ref, mono_ref.shape[1], cells, fold
+    )
+    kept = len(exponent_rows())
+    packed_ref[9 * kept :, :] = jnp.zeros((packed_ref.shape[0] - 9 * kept, TILE), jnp.float32)
+    for k in range(9):
+        packed_ref[k * kept : (k + 1) * kept, :] = total[k * MONO_ROWS : k * MONO_ROWS + kept]
+    turned = packed_ref[...].T
+    blocks, wide = out_ref.shape[0], out_ref.shape[1] // cells
+    for block in range(blocks):
+        for part in range(wide):
+            out_ref[block, part * cells : (part + 1) * cells, :] = turned[
+                block * cells : (block + 1) * cells, part * TILE : (part + 1) * TILE
+            ]
+    for copy in copies:
+        copy.wait()
+
+
+def return_kernel(part_ref, force_ref, moment_ref, held_ref, turn_ref, send_sem, recv_sem):
+    offsets = owners(lax.axis_size("dx"))
+    home = offsets.index((0, 0))
+    away = [n for n in range(len(offsets)) if n != home]
+    greeted = [offsets[n] for n in away]
+    greet(greeted)()
+    copies = start_copies(
+        greeted, lambda n: part_ref.at[away[n]], lambda n: held_ref.at[n], send_sem, recv_sem
+    )
+    total = part_ref[home]
+    for n, copy in enumerate(copies):
+        copy.wait()
+        total = total + held_ref[n]
+    for m in range(3):
+        for q in range(4):
+            row = 4 * m + q
+            force_ref[m : m + 1, q * TILE : (q + 1) * TILE] = total[row : row + 1]
+    cells = moment_ref.shape[1]
+    wide = (total.shape[0] - NODE_ROWS) // cells
+    for part in range(wide):
+        first = NODE_ROWS + part * cells
+        turn_ref[part * TILE : (part + 1) * TILE, :] = total[first : first + cells].T
+    moment_ref[...] = turn_ref[: moment_ref.shape[0], :]
+
+
+def spread(rows, source_ref, index):
+    columns = rows.T
     for q in range(6):
         source_ref[index, q] = jnp.broadcast_to(columns[:, q : q + 1], (TILE, TILE))
 
@@ -106,32 +205,28 @@
 
 
 def force_kernel(
-    list_ref, count_ref, mid_ref, line_ref, burgers_ref, node_ref, ghost_ref, out_ref,
-    source_ref, force_ref,
+    fold, list_ref, count_ref, mid_ref, line_ref, burgers_ref, node_ref, ghost_ref, cell_ref,
+    out_ref, source_ref, force_ref,
 ):
     own_count = mid_ref.shape[1] // TILE
-    ghost_slots = ghost_ref.shape[0] // 8
+    slots = ghost_ref.shape[1]
 
     def spread_own(tile, carry):
         cols = pl.ds(pl.multiple_of(tile * TILE, TILE), TILE)
-        spread(
-            rows_of(mid_ref, cols), rows_of(line_ref, cols), rows_of(burgers_ref, cols),
-            source_ref, tile,
-        )
+        moment = cross(rows_of(burgers_ref, cols), rows_of(line_ref, cols))
+        rows = rows_of(mid_ref, cols) + [shear_scale * row for row in moment]
+        rows = rows + [jnp.zeros((2, TILE), jnp.float32)]
+        spread(jnp.concatenate(rows, axis=0), source_ref, tile)
         return carry
 
-    lax.fori_loop(0, own_count, spread_own, 0, unroll=2)
-
-    def spread_ghost(slot, carry):
-        q = slot // ghost_slots
-        d = q + jnp.where(q >= 4, 1, 0)
-        shift = ((d // 3 - 1).astype(jnp.float32), (d % 3 - 1).astype(jnp.float32), 0.0)
-        rows = [ghost_ref[slot, r : r + 1, :] for r in range(9)]
-        mid = [rows[axis] + shift[axis] for axis in range(3)]
-        spread(mid, rows[3:6], rows[6:9], source_ref, own_count + slot)
+    lax.fori_loop(0, own_count, spread_own, 0, unroll=4)
+
+    def spread_ghost(group, carry):
+        for slot in range(slots):
+            spread(ghost_ref[group, slot], source_ref, own_count + group * slots + slot)
         return carry
 
-    lax.fori_loop(0, 8 * ghost_slots, spread_ghost, 0, unroll=2)
+    lax.fori_loop(0, 8, spread_ghost, 0, unroll=2)
 
     def one_tile(tile, carry):
         cols = pl.ds(pl.multiple_of(tile * TILE, TILE), TILE)
@@ -196,7 +291,7 @@
         for end in range(2):
             node = node_ref[end : end + 1, cols]
             member = jnp.where(lanes == node % TILE, 1.0, 0.0).astype(jnp.bfloat16)
-            block = node // TILE - place
+            block = folded(node // TILE, quads, fold) - place
             left = []
             for value in (high, low):
                 for d in range(directions):
@@ -210,7 +305,9 @@
         jnp.zeros((2 * directions * NODE_ROWS, TILE), jnp.float32),
     )
     half = directions * NODE_ROWS
-    out_ref[...] = (total[:half] + total[half:]).reshape(out_ref.shape)
+    total = (total[:half] + total[half:]).reshape(directions, NODE_ROWS, TILE)
+    out_ref[:, :NODE_ROWS, :] = total
+    out_ref[:, NODE_ROWS:, :] = cell_ref[...]
 
 
 def vmem():
@@ -221,38 +318,77 @@
     return pl.BlockSpec(memory_space=pltpu.SMEM)
 
 
-def cells_call(mid, line, burgers, cell, cell_rows):
+def pack_call(lists, counts, mid, line, burgers):
     return pl.pallas_call(
-        cells_kernel,
-        out_shape=jax.ShapeDtypeStruct((cell_rows, 3 * TILE), jnp.float32),
-        in_specs=[vmem()] * 4,
+        pack_kernel,
+        out_shape=jax.ShapeDtypeStruct((8, lists.shape[1], 8, TILE), jnp.float32),
+        in_specs=[smem()] * 2 + [vmem()] * 3,
         out_specs=vmem(),
-        scratch_shapes=[pltpu.VMEM((MONO_ROWS, 4 * TILE), jnp.float32)],
         compiler_params=pltpu.CompilerParams(vmem_limit_bytes=16 << 20),
-        cost_estimate=pl.CostEstimate(flops=10**9, bytes_accessed=10**6, transcendentals=0),
-    )(mid, line, burgers, cell)
-
-
-def force_call(pairs, counts, mid, line, burgers, node, ghosts):
-    pool = mid.shape[1] // TILE + ghosts.shape[0]
+    )(lists, counts, mid, line, burgers)
+
+
+def ghost_call(packets, mid, line, burgers, cell, cells, blocks):
+    fold = blocks == 6
+    slots = packets.shape[1]
+    wide = pl.cdiv(9 * len(exponent_rows()), TILE)
     return pl.pallas_call(
-        force_kernel,
-        out_shape=jax.ShapeDtypeStruct((9, NODE_ROWS, TILE), jnp.float32),
-        in_specs=[smem()] * 2 + [vmem()] * 5,
+        functools.partial(ghost_kernel, cells, fold),
+        out_shape=(
+            jax.ShapeDtypeStruct((8, slots, 8, TILE), jnp.float32),
+            jax.ShapeDtypeStruct((blocks, wide * cells, TILE), jnp.float32),
+        ),
+        in_specs=[vmem()] * 5,
+        out_specs=(vmem(), vmem()),
+        scratch_shapes=[
+            pltpu.VMEM((MONO_ROWS, 4 * TILE), jnp.float32),
+            pltpu.VMEM((wide * TILE, TILE), jnp.float32),
+            pltpu.SemaphoreType.DMA((8,)),
+            pltpu.SemaphoreType.DMA((8,)),
+        ],
+        compiler_params=pltpu.CompilerParams(
+            collective_id=0, has_side_effects=True, vmem_limit_bytes=16 << 20
+        ),
+    )(packets, mid, line, burgers, cell)
+
+
+def force_call(pairs, counts, mid, line, burgers, node, ghosts, cell_part):
+    pool = mid.shape[1] // TILE + ghosts.shape[0] * ghosts.shape[1]
+    blocks, rows, _ = cell_part.shape
+    return pl.pallas_call(
+        functools.partial(force_kernel, blocks == 6),
+        out_shape=jax.ShapeDtypeStruct((blocks, NODE_ROWS + rows, TILE), jnp.float32),
+        in_specs=[smem()] * 2 + [vmem()] * 6,
         out_specs=vmem(),
         scratch_shapes=[
             pltpu.VMEM((pool, 6, TILE, TILE), jnp.float32),
             pltpu.VMEM((3, mid.shape[1]), jnp.float32),
         ],
         compiler_params=pltpu.CompilerParams(vmem_limit_bytes=40 << 20),
-    )(pairs, counts, mid, line, burgers, node, ghosts)
-
-
-def returned(grid):
-    rows = [passed_along(grid[row], "dx", stride) for stride, row in ((1, 2), (-1, 0))]
-    middle = grid[1] + rows[0] + rows[1]
-    columns = [passed_along(middle[col], "dy", stride) for stride, col in ((1, 2), (-1, 0))]
-    return middle[1] + columns[0] + columns[1]
+    )(pairs, counts, mid, line, burgers, node, ghosts, cell_part)
+
+
+def return_call(parts, cells):
+    blocks, rows, _ = parts.shape
+    wide = (rows - NODE_ROWS) // cells
+    return pl.pallas_call(
+        return_kernel,
+        out_shape=(
+            jax.ShapeDtypeStruct((3, 4 * TILE), jnp.float32),
+            jax.ShapeDtypeStruct((9 * len(exponent_rows()), cells), jnp.float32),
+        ),
+        in_specs=[vmem()],
+        out_specs=(vmem(), vmem()),
+        scratch_shapes=[
+            pltpu.VMEM((blocks - 1, rows, TILE), jnp.float32),
+            pltpu.VMEM((wide * TILE, cells), jnp.float32),
+            pltpu.SemaphoreType.DMA((blocks - 1,)),
+            pltpu.SemaphoreType.DMA((blocks - 1,)),
+        ],
+        compiler_params=pltpu.CompilerParams(
+            collective_id=1, has_side_effects=True, vmem_limit_bytes=16 << 20
+        ),
+    )(parts)
 
 
 def on_device(
@@ -260,31 +396,14 @@
     ghost_list, ghost_count, pair_list, pair_count,
 ):
     mid, line, burgers = seg_mid[0, 0], seg_line[0, 0], seg_burgers[0, 0]
-    cells = 8
-    seg_data = jnp.concatenate([mid, line, burgers], axis=0)
-    own_tiles = seg_data.reshape(9, -1, TILE).transpose(1, 0, 2)
-    slots = ghost_list.shape[3]
-    packets = own_tiles[ghost_list[0, 0]]
-    valid = jnp.arange(slots, dtype=jnp.int32)[None, :] < ghost_count[0, 0][:, None]
-    packets = packets * valid.astype(jnp.float32)[:, :, None, None]
-    from_left = passed_along(packets[5:8], "dx", 1)
-    from_right = passed_along(packets[0:3], "dx", -1)
-    upward = jnp.stack([packets[4], from_left[2], from_right[2]])
-    downward = jnp.stack([packets[3], from_left[0], from_right[0]])
-    from_below = passed_along(upward, "dy", 1)
-    from_above = passed_along(downward, "dy", -1)
-    groups = [
-        from_below[1], from_left[1], from_above[1], from_below[0],
-        from_above[0], from_below[2], from_right[1], from_above[2],
-    ]
-    ghosts = jnp.concatenate(groups, axis=0)
-    cell_part = cells_call(mid, line, burgers, seg_cell[0], 9 * cells)
-    cell_sum = returned(cell_part.reshape(3, 3, cells, -1))
-    moments = cell_sum[:, : 9 * MONO_ROWS].reshape(cells, 9, MONO_ROWS)
-    moments = moments[:, :, : len(exponent_rows())].reshape(cells, -1).T
-    node_part = force_call(pair_list[0, 0], pair_count[0, 0, :], mid, line, burgers, seg_node[0, 0], ghosts)
-    node_sum = returned(node_part.reshape(3, 3, NODE_ROWS, TILE))
-    force = node_sum[:12].reshape(3, 4 * TILE)
+    cells = CELL_DEV
+    blocks = len(owners(lax.axis_size("dx")))
+    packets = pack_call(ghost_list[0, 0], ghost_count[0, 0], mid, line, burgers)
+    ghosts, cell_part = ghost_call(packets, mid, line, burgers, seg_cell[0], cells, blocks)
+    parts = force_call(
+        pair_list[0, 0], pair_count[0, 0], mid, line, burgers, seg_node[0, 0], ghosts, cell_part
+    )
+    force, moments = return_call(parts, cells)
     return (force[None, None], moments)
 
 

time: 70.7 us -> 58.5 us (0.83)
  starting transfers between devices: 21.8 us -> 0 us
  Pallas kernels: 37.1 us -> 52.7 us
  local copies, waits for them, and re-layouts: 7.36 us -> 4.4 us
  waiting for transfers between devices: 2.35 us -> 0 us
    ppermute x12 -> x0, starting transfers between devices: 21.8 us -> none  [passed_along(): return lax.ppermute(block, axis, route)]
    pallas_call x2 -> x4, Pallas kernels: 37.1 us -> 52.7 us  [the longest x1 36 us: force_call(): pl.pallas_call(functools.partial(force_kernel, blocks == 6), out_shape=ja...]
    ppermute x12 -> x0, waiting for transfers between devices: 2.35 us -> none  [passed_along(): return lax.ppermute(block, axis, route)]
    concatenate x4 -> x0, local copies, waits for them, and re-layouts: 0.92 us -> none  [the longest x3 0.92 us: on_device(): seg_data = jnp.concatenate([mid, line, burgers], axis=0)]
    reshape x2 -> x0, local copies, waits for them, and re-layouts: 0.76 us -> none  [the longest x1 0.68 us: on_device(): moments = moments[:, :, :len(exponent_rows())].reshape(cells, -1).T]
    unnamed x28 -> x21, local copies, waits for them, and re-layouts: 4.3 us -> 4.31 us
  transfers between devices with their start and end apart: 12 -> 0, of which waited for: 2 -> 0; matrix products, arithmetic and copies ran while one was open for 1% -> 0% of each run, Pallas kernels for 3% -> 0%
where the time goes in v2:
time: 58.5 us; the launch traced here: 57.9 us
  Pallas kernels  52.7 us (90%)
  local copies, waits for them, and re-layouts  4.4 us (8%)
  between operations  0.73 us (1%)
    pallas_call x1, Pallas kernels, force_call(): pl.pallas_call(functools.partial(force_kernel, blocks == 6), out_shape=ja...  36 us
    pallas_call x1, Pallas kernels, ghost_call(): pl.pallas_call(functools.partial(ghost_kernel, cells, fold), out_shape=(j...  8.98 us
    pallas_call x1, Pallas kernels, return_call(): pl.pallas_call(return_kernel, out_shape=(jax.ShapeDtypeStruct((3, 4 * TIL...  7.1 us
    unnamed x21, local copies, waits for them, and re-layouts  4.31 us

profile of v2, /device:TPU:0, one launch (start us, length us, event | category | flops | bytes accessed | tf_op | source)
XLA Modules:
  0.0 57.9 jit_solution(16123405247679523860)
XLA Ops:
  0.6 0.0 copy-start.6
  0.6 0.0 copy-start.7
  0.6 0.7 %copy-done.7 = s32[1,1,8,2]{2,3,1,0:T(2,128)S(1)} copy-done((s32[1,1,8,2]{2,3,1,0:T(2,128)S(1)}, s32[1,1,8,2]{2,3,1,0:T(2,128)}, u32[]{:S(2)}) %copy-start.7) | copy-done | bytes 88
  1.3 0.1 copy.12.list_ref
  1.4 0.0 copy-done.6
  1.4 0.1 copy.11
  1.5 0.0 copy-start.4
  1.5 0.0 copy-start.5
  1.5 0.8 %copy.21 = f32[1,1,3,4096]{3,2,1,0:T(4,128)S(1)} copy(f32[1,1,3,4096]{3,1,2,0:T(1,128)} %param.9) | data formatting | bytes 98304
  2.3 0.0 copy-done.4
  2.4 0.0 copy-done.5
  2.4 0.1 copy_bitcast_fusion
  2.4 0.0 copy-start.2
  2.5 0.6 %copy-done.2 = s32[1,1,8]{2,1,0:T(1,128)S(1)} copy-done((s32[1,1,8]{2,1,0:T(1,128)S(1)}, s32[1,1,8]{2,1,0:T(1,128)}, u32[]{:S(2)}) %copy-start.2) | copy-done | bytes 56
  3.1 0.7 %shard_map.104.packet_ref = f32[8,2,8,128]{3,2,1,0:T(8,128)S(1)} custom-call(s32[8,2]{1,0:T(8,128)S(1)} %copy.12.list_ref, s32[8]{0:T(128)S(1)} %bitcast.21, f32[3,4096]{1,0:T(4,128)S(1)} %bitcast.14, f32[3,4096]{1,0:T(4,128)S(1)} %get-tuple-element.13.line_ref, f32[3,4096]{1,0:T(4,128)S(1)} %get-tuple-element.12.burgers_ref), custom_call_target="tpu_custom_call" | custom-call | tf_op jit(solution)/shard_map/pallas_call | solution.py:322
  3.8 0.0 copy-done.1
  3.8 9.0 %shard_map.105 = (f32[8,2,8,128]{3,2,1,0:T(8,128)S(1)}, f32[6,24,128]{2,1,0:T(8,128)S(1)}) custom-call(f32[8,2,8,128]{3,2,1,0:T(8,128)S(1)} %shard_map.104.packet_ref, f32[3,4096]{1,0:T(4,128)S(1)} %bitcast.15, f32[3,4096]{1,0:T(4,128)S(1)} %get-tuple-element.13.line_ref, f32[3,4096]{1,0:T(4,128)S(1)} %get-tuple-element.12.burgers_ref, s32[1,4096]{1,0:T(1,128)S(1)} %bitcast.19), custom_call_target="tpu_custom_call" | custom-call | tf_op jit(solution)/shard_map/pallas_call | solution.py:335
  12.8 0.0 copy-start.3
  12.8 0.0 copy-done
  12.8 0.6 %copy-done.3 = s32[1,1,32]{2,1,0:T(1,128)S(1)} copy-done((s32[1,1,32]{2,1,0:T(1,128)S(1)}, s32[1,1,32]{2,1,0:T(1,128)}, u32[]{:S(2)}) %copy-start.3) | copy-done | bytes 152
  13.5 36.0 %shard_map.106.part_ref = f32[6,40,128]{2,1,0:T(8,128)S(1)} custom-call(s32[32,12]{1,0:T(8,128)S(1)} %bitcast.17, s32[32]{0:T(128)S(1)} %bitcast.22, f32[3,4096]{1,0:T(4,128)S(1)} %bitcast.16, f32[3,4096]{1,0:T(4,128)S(1)} %get-tuple-element.13.line_ref, f32[3,4096]{1,0:T(4,128)S(1)} %get-tuple-element.12.burgers_ref, s32[2,4096]{1,0:T(2,128)S(1)} %bitcast.18, ...), custom_call_target="tpu_custom_call" | custom-call | tf_op jit(solution)/shard_map/pallas_call | solution.py:358
  49.5 7.1 %shard_map.107 = (f32[3,512]{1,0:T(4,128)S(1)}, f32[315,8]{1,0:T(8,128)S(1)}) custom-call(f32[6,40,128]{2,1,0:T(8,128)S(1)} %shard_map.106.part_ref), custom_call_target="tpu_custom_call" | custom-call | tf_op jit(solution)/shard_map/pallas_call | solution.py:374
  56.6 0.6 %copy.13 = f32[1,1,3,512]{3,1,2,0:T(1,128)} copy(f32[1,1,3,512]{3,2,1,0:T(4,128)S(1)} %bitcast.20) | data formatting | bytes 12288
  57.2 0.7 %copy.14 = f32[315,8]{0,1:T(8,128)} copy(f32[315,8]{1,0:T(8,128)S(1)} %get-tuple-element.11) | data formatting | bytes 20160
  (2 shorter events, 0.0 us)
Async XLA Ops:
  0.6 0.8 %copy-start.6 = (s32[1,1,32,12]{2,1,3,0:T(1,128)S(1)}, s32[1,1,32,12]{2,1,3,0:T(1,128)}, u32[]{:S(2)}) copy-start(s32[1,1,32,12]{2,1,3,0:T(1,128)} %param.16) | copy-start | bytes 4612
  0.6 0.7 %copy-start.7 = (s32[1,1,8,2]{2,3,1,0:T(2,128)S(1)}, s32[1,1,8,2]{2,3,1,0:T(2,128)}, u32[]{:S(2)}) copy-start(s32[1,1,8,2]{2,3,1,0:T(2,128)} %param.14) | copy-start | bytes 196
  1.5 0.8 %copy-start.4 = (f32[1,1,3,4096]{3,1,2,0:T(1,128)S(1)}, f32[1,1,3,4096]{3,1,2,0:T(1,128)}, u32[]{:S(2)}) copy-start(f32[1,1,3,4096]{3,1,2,0:T(1,128)} %param.11) | copy-start | bytes 147460
  1.5 0.9 %copy-start.5 = (f32[1,1,3,4096]{3,1,2,0:T(1,128)S(1)}, f32[1,1,3,4096]{3,1,2,0:T(1,128)}, u32[]{:S(2)}) copy-start(f32[1,1,3,4096]{3,1,2,0:T(1,128)} %param.10) | copy-start | bytes 147460
  2.4 0.7 %copy-start.2 = (s32[1,1,8]{2,1,0:T(1,128)S(1)}, s32[1,1,8]{2,1,0:T(1,128)}, u32[]{:S(2)}) copy-start(s32[1,1,8]{2,1,0:T(1,128)} %param.15) | copy-start | bytes 100
  3.1 0.7 %copy-start.1 = (s32[1,1,4096]{2,1,0:T(1,128)S(1)}, s32[1,1,4096]{2,1,0:T(1,128)}, u32[]{:S(2)}) copy-start(s32[1,1,4096]{2,1,0:T(1,128)} %param.12) | copy-start | bytes 49156
  3.8 9.0 %copy-start = (s32[1,1,2,4096]{3,2,1,0:T(2,128)S(1)}, s32[1,1,2,4096]{3,2,1,0:T(2,128)}, u32[]{:S(2)}) copy-start(s32[1,1,2,4096]{3,2,1,0:T(2,128)} %param.13) | copy-start | bytes 98308
  12.8 0.7 %copy-start.3 = (s32[1,1,32]{2,1,0:T(1,128)S(1)}, s32[1,1,32]{2,1,0:T(1,128)}, u32[]{:S(2)}) copy-start(s32[1,1,32]{2,1,0:T(1,128)} %param.17) | copy-start | bytes 388
